TPU v7x, 256 devices: a whole 4x4x8 slice. The times are simulated.
256 devices in a mesh: row: 32 (over y, z), col: 8 (over x, core).
Axes of the slice: x: 4, y: 4, z: 8, core: 2. Of those that a mesh axis runs over, the one named last changes fastest.
Arguments:
- points: float32 [16, 32768], P(None, ('col', 'row')), may hold values from -5 to 5
- inv_scales: float32 [16], replicated, may hold values from 0.1 to 0.4
- amplitude: float32 [1], replicated, may hold values from 0.5 to 2
- noise_var: float32 [1], replicated, may hold values from 0.3 to 1
- targets: float32 [8, 32768], P(None, ('col', 'row')), may hold values from -6 to 6
- initial: float32 [8, 32768], P(None, ('col', 'row')), may hold values from -3 to 3
- ritz_basis: float32 [64, 32768], P(None, ('col', 'row')), may hold values from -0.03125 to 0.03125
Outputs:
- solution: float32 [8, 32768], P(None, ('col', 'row'))
- residual: float32 [8, 32768], P(None, ('col', 'row'))
All inputs are finite; a program needn't handle non-finite values.
Results may differ from a plain program's by a relative error of at most 0.00065.
Values sent between devices are 32-bit elements; how exact they have to be, the bound alone decides.
A program may use at most 128 MiB of HBM per device.

v0:
```python
import jax
import jax.numpy as jnp
from jax import lax
from jax.sharding import Mesh
from jax.sharding import PartitionSpec as P

ITERS = 1
ROW = ("row_0", "row_1")
COL = ("col_0", "col_1")
COL_ROW = ("col_0", "col_1", "row_0", "row_1")


HIGH = lax.Precision.HIGHEST


def laid_out(pieces, dim):
    dims = list(pieces.shape[1:])
    dims[dim] *= pieces.shape[0]
    return jnp.moveaxis(pieces, 0, dim).reshape(dims)


def from_everyone(array, axis):
    copies = jnp.broadcast_to(array, (lax.axis_size(axis), *array.shape))
    return lax.all_to_all(copies, axis, split_axis=0, concat_axis=0, tiled=True)


def gathered_copies(array, axis, dim):
    return laid_out(from_everyone(array, axis), dim)


def split_up(array, dim, peers):
    dims = array.shape
    pieces = array.reshape(*dims[:dim], peers, dims[dim] // peers, *dims[dim + 1 :])
    return jnp.moveaxis(pieces, dim, 0)


def sum_at_owner(array, axis, dim):
    pieces = split_up(array, dim, lax.axis_size(axis))
    arrived = lax.all_to_all(pieces, axis, split_axis=0, concat_axis=0, tiled=True)
    return arrived.sum(axis=0)


def taken_together(array, axis):
    everything = from_everyone(array, axis)
    return jnp.sum(everything, axis=0)


def one_axis_at_a_time(array, axes):
    far, near = axes
    return taken_together(taken_together(array, near), far)


def in_one(arrays, axis):
    flat, at, gathered = (jnp.concatenate([a.reshape(-1) for a in arrays]), 0, [])
    subtotal = one_axis_at_a_time(flat, axis)
    for a in arrays:
        gathered.append(subtotal[at : at + a.size].reshape(a.shape))
        at += a.size
    return tuple(gathered)


def kernel_tile(col_x, col_sq, row_x, row_sq, gain):
    cross_term = jnp.dot(col_x.T, row_x, precision=HIGH, preferred_element_type=jnp.float32)
    distance = jnp.maximum(col_sq[:, None] + row_sq[None, :] - 2.0 * cross_term, 0.0)
    return gain * jnp.exp(-0.5 * distance)


def coarse_solve(factor, rhs_block):
    middle = lax.linalg.triangular_solve(factor, rhs_block, left_side=True, lower=True)
    return lax.linalg.triangular_solve(factor, middle, left_side=True, lower=True, transpose_a=True)


def matmul(left, right):
    return jnp.dot(left, right, precision=HIGH, preferred_element_type=jnp.float32)


def local(points, inv_scales, amplitude, noise_var, targets, initial, ritz_basis):
    gain = amplitude[0]
    nugget = noise_var[0]
    row_x = gathered_copies(points, ROW, 1) * inv_scales[:, None]
    row_sq = jnp.sum(row_x * row_x, axis=0)
    near_x = gathered_copies(points, COL, 1) * inv_scales[:, None]
    near_sq = jnp.sum(near_x * near_x, axis=0)

    def apply_operator(vectors):
        partial_value = matmul(
            gathered_copies(vectors, COL, 1), kernel_tile(near_x, near_sq, row_x, row_sq, gain)
        )
        return sum_at_owner(partial_value, ROW, 1) + nugget * vectors

    rhs_count = initial.shape[0]
    applied_all = apply_operator(jnp.concatenate([initial, ritz_basis], 0))
    ritz_image = applied_all[rhs_count:]
    first_residual = targets - applied_all[:rhs_count]
    coarse, projected = in_one(
        (matmul(ritz_basis, ritz_image.T), matmul(ritz_basis, first_residual.T)),
        (("row_0", "row_1"), ("col_0", "col_1")),
    )
    coarse = 0.5 * (coarse + coarse.T)
    factor = jnp.linalg.cholesky(coarse)
    coarse_inverse = coarse_solve(factor, jnp.eye(coarse.shape[0], dtype=jnp.float32))
    amounts = matmul(coarse_inverse, projected)
    solution = initial + matmul(amounts.T, ritz_basis)
    residual = first_residual - matmul(amounts.T, ritz_image)

    def residual_stats(current):
        return in_one(
            (matmul(ritz_image, current.T), jnp.sum(current * current, axis=1)),
            (("row_0", "row_1"), ("col_0", "col_1")),
        )

    against, sq_norm = residual_stats(residual)
    direction = residual - matmul(matmul(coarse_inverse, against).T, ritz_basis)

    def plain_step(step, state):
        solution, residual, direction, sq_norm = state
        applied = apply_operator(direction)
        curvature = one_axis_at_a_time(
            jnp.sum(direction * applied, axis=1), (("row_0", "row_1"), ("col_0", "col_1"))
        )
        step_size = sq_norm / curvature
        solution = solution + step_size[:, None] * direction
        residual = residual - step_size[:, None] * applied
        against, new_norm = residual_stats(residual)
        correction = matmul(matmul(coarse_inverse, against).T, ritz_basis)
        direction = residual + (new_norm / sq_norm)[:, None] * direction - correction
        return (solution, residual, direction, new_norm)

    solution, residual, direction, sq_norm = lax.fori_loop(
        0, ITERS, plain_step, (solution, residual, direction, sq_norm)
    )
    return (solution, residual)


def solution(mesh):
    torus = Mesh(mesh.devices.reshape(4, 8, 4, 2), ("row_0", "row_1", "col_0", "col_1"))
    in_specs = (
        P(None, COL_ROW),
        P(),
        P(),
        P(),
        P(None, COL_ROW),
        P(None, COL_ROW),
        P(None, COL_ROW),
    )
    out_specs = (P(None, COL_ROW), P(None, COL_ROW))
    return jax.shard_map(local, mesh=torus, in_specs=in_specs, out_specs=out_specs, check_vma=False)
```

profile of v0, /device:TPU:1, one launch (start us, length us, event | category | flops | bytes accessed | tf_op | source)
XLA Modules:
  0.0 255.8 jit_solution(16806615343434934951)
XLA Ops:
  0.6 1.3 broadcast_in_dim.53
  2.0 6.5 %all-to-all-start.1 = ((f32[8,16,128]{2,1,0:T(8,128)}), f32[8,16,128]{2,1,0:T(8,128)S(1)}, u32[]{:S(2)}, u32[]{:S(2)}) async-start(f32[8,16,128]{2,1,0:T(8,128)} %broadcast_in_dim.53), calls=%async_computation.1 | async-start | bytes 131072 | tf_op jit(solution)/shard_map/all_to_all | solution.py:24
  9.9 3.4 %all-to-all-done.1 = f32[8,16,128]{2,1,0:T(8,128)S(1)} async-done(((f32[8,16,128]{2,1,0:T(8,128)}), f32[8,16,128]{2,1,0:T(8,128)S(1)}, u32[]{:S(2)}, u32[]{:S(2)}) %all-to-all-start.1) | async-done | bytes 65568 | tf_op jit(solution)/shard_map/all_to_all | solution.py:24
  13.3 10.4 %all_to_all.74 = f32[8,72,128]{2,1,0:T(8,128)S(1)} all-to-all(f32[8,72,128]{2,1,0:T(8,128)S(1)} %broadcast_in_dim.52), channel_id=1, replica_groups=mesh['row_0'=4,'row_1'=8,'col_0'=4,'col_1'=2] {'col_0','col_1'}, dimensions={0} | all-to-all | bytes 589824 | tf_op jit(solution)/shard_map/all_to_all | solution.py:24
  23.7 1.4 broadcast_in_dim.54
  25.1 10.5 %all-to-all-start.2 = ((f32[32,16,128]{2,1,0:T(8,128)}), f32[32,16,128]{2,1,0:T(8,128)S(1)}, u32[]{:S(2)}, u32[]{:S(2)}) async-start(f32[32,16,128]{2,1,0:T(8,128)} %broadcast_in_dim.54), calls=%async_computation.2 | async-start | bytes 524288 | tf_op jit(solution)/shard_map/all_to_all | solution.py:24
  37.2 8.2 %all-to-all-done.2 = f32[32,16,128]{2,1,0:T(8,128)S(1)} async-done(((f32[32,16,128]{2,1,0:T(8,128)}), f32[32,16,128]{2,1,0:T(8,128)S(1)}, u32[]{:S(2)}, u32[]{:S(2)}) %all-to-all-start.2) | async-done | bytes 262176 | tf_op jit(solution)/shard_map/all_to_all | solution.py:24
  45.3 0.8 fusion.3
  46.1 18.7 %exponential_multiply_fusion = f32[4096,1024]{1,0:T(8,128)S(1)} fusion(f32[4096]{0:T(1024)S(1)} %bitcast.82, f32[1024]{0:T(1024)S(1)} %bitcast.84, f32[]{:T(128)} %bitcast.75, f32[32,16,128]{2,1,0:T(8,128)S(1)} %all-to-all-done.2, f32[16]{0:T(128)} %param.8, f32[8,16,128]{2,1,0:T(8,128)S(1)} %all-to-all-done.1), kind=kOutput, calls=%fused_computation | convolution fusion | flops 830554112 | bytes 17125444 | tf_op jit(solution)/shard_map/dot_general | solution.py:63
  64.9 5.7 %copy-done = f32[4096,1024]{1,0:T(8,128)} copy-done((f32[4096,1024]{1,0:T(8,128)}, f32[4096,1024]{1,0:T(8,128)S(1)}, u32[]{:S(2)}) %copy-start) | copy-done | bytes 16777240
  70.5 17.5 %convolution_bitcast_fusion = f32[32,72,128]{2,1,0:T(8,128)} fusion(f32[72,1024,1]{1,0,2:T(8,128)S(1)} %reshape.134, f32[32,128,1024]{2,1,0:T(8,128)S(1)} %bitcast.79), kind=kOutput, calls=%fused_computation.1 | convolution fusion | flops 3623878656 | bytes 18251776 | tf_op jit(solution)/shard_map/dot_general | solution.py:74
  88.0 6.5 %all-to-all-start.3 = ((f32[32,72,128]{2,1,0:T(8,128)}), f32[32,72,128]{2,1,0:T(8,128)S(1)}, u32[]{:S(2)}, u32[]{:S(2)}) async-start(f32[32,72,128]{2,1,0:T(8,128)} %convolution_bitcast_fusion), calls=%async_computation.3 | async-start | bytes 2359296 | tf_op jit(solution)/shard_map/all_to_all | solution.py:39
  95.2 27.0 %all-to-all-done.3 = f32[32,72,128]{2,1,0:T(8,128)S(1)} async-done(((f32[32,72,128]{2,1,0:T(8,128)}), f32[32,72,128]{2,1,0:T(8,128)S(1)}, u32[]{:S(2)}, u32[]{:S(2)}) %all-to-all-start.3) | async-done | bytes 1179680 | tf_op jit(solution)/shard_map/all_to_all | solution.py:39
  123.1 12.7 %all_to_all.75 = f32[8,1,4608]{2,1,0:T(1,128)S(1)} all-to-all(f32[8,1,4608]{2,1,0:T(1,128)S(1)} %broadcast_in_dim.55), channel_id=1, replica_groups=mesh['row_0'=4,'row_1'=8,'col_0'=4,'col_1'=2] {'col_0','col_1'}, dimensions={0} | all-to-all | bytes 294912 | tf_op jit(solution)/shard_map/all_to_all | solution.py:24
  136.2 20.1 %all_to_all.76 = f32[32,1,4608]{2,1,0:T(1,128)S(1)} all-to-all(f32[32,1,4608]{2,1,0:T(1,128)S(1)} %broadcast_in_dim.56), channel_id=1, replica_groups=mesh['row_0'=4,'row_1'=8,'col_0'=4,'col_1'=2] {'row_0','row_1'}, dimensions={0} | all-to-all | bytes 1179648 | tf_op jit(solution)/shard_map/all_to_all | solution.py:24
  156.9 5.8 %cholesky.17 = f32[64,64]{1,0:T(8,128)S(1)} custom-call(f32[64,64]{1,0:T(8,128)S(1)} %fusion.13), custom_call_target="Cholesky" | custom-call | tf_op jit(solution)/shard_map/jit(cholesky)/cholesky | solution.py:100
  164.1 4.9 %custom-call.8 = f32[1,64,64]{1,2,0:T(8,128)S(1)} custom-call(f32[1,64,64]{2,1,0:T(8,128)S(1)} %fusion.7), custom_call_target="InvertDiagBlocksLowerTriangular" | custom-call | tf_op jit(solution)/shard_map/triangular_solve | solution.py:70
  170.3 10.7 %all_to_all.77 = f32[8,1,520]{2,1,0:T(1,128)S(1)} all-to-all(f32[8,1,520]{2,1,0:T(1,128)S(1)} %broadcast_in_dim.57), channel_id=1, replica_groups=mesh['row_0'=4,'row_1'=8,'col_0'=4,'col_1'=2] {'col_0','col_1'}, dimensions={0} | all-to-all | bytes 33280 | tf_op jit(solution)/shard_map/all_to_all | solution.py:24
  181.0 14.0 %all_to_all.78 = f32[32,1,520]{2,1,0:T(1,128)S(1)} all-to-all(f32[32,1,520]{2,1,0:T(1,128)S(1)} %broadcast_in_dim.58), channel_id=1, replica_groups=mesh['row_0'=4,'row_1'=8,'col_0'=4,'col_1'=2] {'row_0','row_1'}, dimensions={0} | all-to-all | bytes 133120 | tf_op jit(solution)/shard_map/all_to_all | solution.py:24
  195.6 9.2 %all_to_all.79 = f32[8,8,128]{2,1,0:T(8,128)S(1)} all-to-all(f32[8,8,128]{2,1,0:T(8,128)S(1)} %broadcast_in_dim.59), channel_id=1, replica_groups=mesh['row_0'=4,'row_1'=8,'col_0'=4,'col_1'=2] {'col_0','col_1'}, dimensions={0} | all-to-all | bytes 65536 | tf_op jit(solution)/shard_map/while/body/eval_jaxpr/all_to_all | solution.py:24
  204.8 16.2 %convolution_bitcast_fusion.1 = f32[32,8,128]{2,1,0:T(8,128)S(1)} fusion(f32[32,128,1024]{2,1,0:T(8,128)} %bitcast.80, f32[8,8,128]{2,1,0:T(8,128)S(1)} %all_to_all.79), kind=kOutput, calls=%fused_computation.2 | convolution fusion | flops 402653184 | bytes 16941056 | tf_op jit(solution)/shard_map/while/body/eval_jaxpr/dot_general | solution.py:74
  220.9 12.1 %all_to_all.80 = f32[32,8,128]{2,1,0:T(8,128)S(1)} all-to-all(f32[32,8,128]{2,1,0:T(8,128)S(1)} %convolution_bitcast_fusion.1), channel_id=1, replica_groups=mesh['row_0'=4,'row_1'=8,'col_0'=4,'col_1'=2] {'row_0','row_1'}, dimensions={0} | all-to-all | bytes 262144 | tf_op jit(solution)/shard_map/while/body/eval_jaxpr/all_to_all | solution.py:39
  233.2 9.1 %all_to_all.81 = f32[8,1,8]{2,1,0:T(1,128)S(1)} all-to-all(f32[8,1,8]{2,1,0:T(1,128)S(1)} %broadcast_in_dim.60), channel_id=1, replica_groups=mesh['row_0'=4,'row_1'=8,'col_0'=4,'col_1'=2] {'col_0','col_1'}, dimensions={0} | all-to-all | bytes 512 | tf_op jit(solution)/shard_map/while/body/eval_jaxpr/all_to_all | solution.py:24
  242.4 12.0 %all_to_all.82 = f32[32,1,8]{2,1,0:T(1,128)S(1)} all-to-all(f32[32,1,8]{2,1,0:T(1,128)S(1)} %broadcast_in_dim.61), channel_id=1, replica_groups=mesh['row_0'=4,'row_1'=8,'col_0'=4,'col_1'=2] {'row_0','row_1'}, dimensions={0} | all-to-all | bytes 2048 | tf_op jit(solution)/shard_map/while/body/eval_jaxpr/all_to_all | solution.py:24
  (62 shorter events, 9.0 us)
Async XLA Ops:
  2.0 11.3 %all-to-all-start.1 = ((f32[8,16,128]{2,1,0:T(8,128)}), f32[8,16,128]{2,1,0:T(8,128)S(1)}, u32[]{:S(2)}, u32[]{:S(2)}) async-start(f32[8,16,128]{2,1,0:T(8,128)} %broadcast_in_dim.53), calls=%async_computation.1 | async-start | bytes 131072 | tf_op jit(solution)/shard_map/all_to_all | solution.py:24
  25.1 20.2 %all-to-all-start.2 = ((f32[32,16,128]{2,1,0:T(8,128)}), f32[32,16,128]{2,1,0:T(8,128)S(1)}, u32[]{:S(2)}, u32[]{:S(2)}) async-start(f32[32,16,128]{2,1,0:T(8,128)} %broadcast_in_dim.54), calls=%async_computation.2 | async-start | bytes 524288 | tf_op jit(solution)/shard_map/all_to_all | solution.py:24
  64.8 5.7 %copy-start = (f32[4096,1024]{1,0:T(8,128)}, f32[4096,1024]{1,0:T(8,128)S(1)}, u32[]{:S(2)}) copy-start(f32[4096,1024]{1,0:T(8,128)S(1)} %exponential_multiply_fusion) | copy-start | bytes 50331652
  64.8 57.4 %copy-start.1 = (f32[64,128]{1,0:T(8,128)S(1)}, f32[64,128]{1,0:T(8,128)}, u32[]{:S(2)}) copy-start(f32[64,128]{1,0:T(8,128)} %param.13) | copy-start | bytes 98308
  64.8 57.8 %copy-start.2 = (f32[8,128]{1,0:T(8,128)S(1)}, f32[8,128]{1,0:T(8,128)}, u32[]{:S(2)}) copy-start(f32[8,128]{1,0:T(8,128)} %param.11) | copy-start | bytes 12292
  88.0 166.4 %copy-start.3 = (f32[8,128]{1,0:T(8,128)S(1)}, f32[8,128]{1,0:T(8,128)}, u32[]{:S(2)}) copy-start(f32[8,128]{1,0:T(8,128)} %param.12) | copy-start | bytes 12292
  88.0 34.1 %all-to-all-start.3 = ((f32[32,72,128]{2,1,0:T(8,128)}), f32[32,72,128]{2,1,0:T(8,128)S(1)}, u32[]{:S(2)}, u32[]{:S(2)}) async-start(f32[32,72,128]{2,1,0:T(8,128)} %convolution_bitcast_fusion), calls=%async_computation.3 | async-start | bytes 2359296 | tf_op jit(solution)/shard_map/all_to_all | solution.py:39
where the time goes:
time: 257 us; the launch traced here: 256 us
  blocking collectives  110 us (43%)
  matrix products  54.8 us (21%)
  waiting for transfers between devices  38.5 us (15%)
  starting transfers between devices  23.5 us (9%)
  other arithmetic  15.1 us (6%)
  local copies, waits for them, and re-layouts  11.3 us (4%)
    all_to_all x8, blocking collectives, from_everyone(): return lax.all_to_all(copies, axis, split_axis=0, concat_axis=0, tiled=True)  98.2 us
    dot_general x10, matrix products, matmul(): jnp.dot(left, right, precision=HIGH, preferred_element_type=jnp.float32)  35.7 us
    all_to_all x1, waiting for transfers between devices, sum_at_owner(): lax.all_to_all(pieces, axis, split_axis=0, concat_axis=0, tiled=True)  27 us
    dot_general x1, matrix products, kernel_tile(): jnp.dot(col_x.T, row_x, precision=HIGH, preferred_element_type=jnp.float32)  18.7 us
    all_to_all x2, starting transfers between devices, from_everyone(): return lax.all_to_all(copies, axis, split_axis=0, concat_axis=0, tiled=True)  17 us
    all_to_all x1, blocking collectives, sum_at_owner(): lax.all_to_all(pieces, axis, split_axis=0, concat_axis=0, tiled=True)  12.1 us
    all_to_all x2, waiting for transfers between devices, from_everyone(): return lax.all_to_all(copies, axis, split_axis=0, concat_axis=0, tiled=True)  11.6 us
    another operation x3, other arithmetic, local(): factor = jnp.linalg.cholesky(coarse)  6.52 us
  transfers between devices with their start and end apart: 3, of which 3 were waited for; matrix products, arithmetic and copies ran while one was open for 1% of the time, Pallas kernels for 0%

commit v1 on v0

v1 whole, which is shorter than its diff:
```python
import functools
import math

import jax
import jax.numpy as jnp
from jax import lax
from jax.experimental import pallas as pl
from jax.experimental.pallas import tpu as pltpu
from jax.sharding import Mesh
from jax.sharding import PartitionSpec as P

F32 = jnp.float32
BF16 = jnp.bfloat16
HIGH = lax.Precision.HIGHEST
MESH = pl.DeviceIdType.MESH
NY, NZ, NX, NC = 4, 8, 4, 2
NF = NX * NY * NC
NG = NX * NC
NQ = NY * NZ
BLK = 128
FEAT = 16
RITZ = 64
RHS = 8
VEC = RITZ + RHS
PAD = 80
NJ = NF * BLK
NPAIR = NZ // 2
STEPS = 16
CHUNK = NJ * NPAIR // STEPS
PER_PAIR = NJ // CHUNK
LOG2E = 1.4426950408889634


def split3(a):
    high = a.astype(BF16).astype(F32)
    rest = a - high
    mid = rest.astype(BF16).astype(F32)
    low = (rest - mid).astype(BF16).astype(F32)
    return high, mid, low


def matmul(a, b, dims):
    return lax.dot_general(a, b, (dims, ((), ())), precision=HIGH, preferred_element_type=F32)


def fast(a, b):
    return jnp.dot(a, b, preferred_element_type=F32)


def features(y, left):
    h, m, low = split3(y)
    sh, sm, sl = split3(-0.5 * jnp.sum(y * y, axis=0, keepdims=True))
    row = lax.broadcasted_iota(jnp.int32, (FEAT, BLK), 0)
    at = 0 if left else 3
    ones = (row < 6) & ((row >= 3) if left else (row < 3))
    extra = jnp.where(row == at, sh, jnp.where(row == at + 1, sm, jnp.where(row == at + 2, sl, 0.0)))
    extra = jnp.where(ones, 1.0, extra)
    zero = jnp.zeros((FEAT, BLK), F32)
    parts = [h, m, h, low, h, m, extra, zero] if left else [h, h, m, h, low, m, extra, zero]
    return jnp.concatenate(parts, axis=0)


def body(
    gain_ref, nugget_ref, scales_ref, points_ref, targets_ref, initial_ref, ritz_ref, out_ref, res_ref,
    px, xf, xz, vf, wz, tgt, ljt, riz, khi, klo, vcat, part, pin, ars, ara, arb, arc, df, dz, fs, fr, gf, dcat,
    sem_in, rx, rxz, rv, rvf, rw, rp, ra, rb, rc, rd, rdz, rf, rg,
    sx, sxz, sv, svf, sw, sp, sa, sb, sc, sd, sdz, sf, sg,
):
    y = lax.axis_index("row_0")
    z = lax.axis_index("row_1")
    x = lax.axis_index("col_0")
    c = lax.axis_index("col_1")
    chip = x * NY + y
    f = chip * NC + c
    g = x * NC + c
    q = y * NZ + z

    def xyc(k):
        o = lax.rem(f + k, NF)
        return {"row_0": lax.rem(o // NC, NY), "row_1": z, "col_0": o // (NC * NY), "col_1": lax.rem(o, NC)}

    def at_z(o):
        return {"row_0": y, "row_1": o, "col_0": x, "col_1": c}

    def remote(src, dst, send, recv, device):
        return pltpu.make_async_remote_copy(
            src_ref=src, dst_ref=dst, send_sem=send, recv_sem=recv, device_id=device, device_id_type=MESH
        )

    def settle(ref, sem):
        pltpu.make_async_copy(ref, ref, sem).wait()

    loads = [
        pltpu.make_async_copy(points_ref, px, sem_in.at[0]),
        pltpu.make_async_copy(ritz_ref, vf.at[f, pl.ds(0, RITZ)], sem_in.at[1]),
        pltpu.make_async_copy(initial_ref, vf.at[f, pl.ds(RITZ, RHS)], sem_in.at[2]),
        pltpu.make_async_copy(targets_ref, tgt, sem_in.at[3]),
        pltpu.make_async_copy(ritz_ref, wz.at[:, pl.ds(pl.multiple_of(z * BLK, BLK), BLK)], sem_in.at[4]),
    ]
    for load in loads:
        load.start()
    barrier = pltpu.get_barrier_semaphore()

    @pl.loop(1, NF)
    def _(k):
        pl.semaphore_signal(barrier, inc=1, device_id=xyc(k), device_id_type=MESH)

    @pl.loop(1, NZ)
    def _(k):
        pl.semaphore_signal(barrier, inc=1, device_id=at_z(lax.rem(z + k, NZ)), device_id_type=MESH)

    gain = gain_ref[0]
    nugget = nugget_ref[0]
    row = lax.broadcasted_iota(jnp.int32, (FEAT, BLK), 0)
    scale = jnp.zeros((FEAT, BLK), F32)
    for i in range(FEAT):
        scale = jnp.where(row == i, scales_ref[i], scale)
    loads[0].wait()
    scaled = px[...] * scale * math.sqrt(LOG2E)
    xf[f] = scaled
    xz[z] = scaled
    for load in loads[1:]:
        load.wait()
    pl.semaphore_wait(barrier, NF - 1 + NZ - 1)

    @pl.loop(1, NF)
    def _(k):
        remote(xf.at[f], xf.at[f], sx, rx, xyc(k)).start()

    @pl.loop(1, NZ)
    def _(k):
        remote(xz.at[z], xz.at[z], sxz, rxz, at_z(lax.rem(z + k, NZ))).start()

    @pl.loop(1, NX * NY)
    def _(k):
        remote(vf.at[f], vf.at[f], sv, rv.at[k], xyc(k * NC)).start()

    own_w = wz.at[:, pl.ds(pl.multiple_of(z * BLK, BLK), BLK)]

    @pl.loop(1, NZ)
    def _(k):
        remote(own_w, own_w, sw, rw, at_z(lax.rem(z + k, NZ))).start()

    settle(xf.at[pl.ds(0, NF - 1)], rx)

    @pl.loop(0, NF)
    def _(j):
        ljt[pl.ds(pl.multiple_of(j * BLK, BLK), BLK), :] = features(xf[j], True).T.astype(BF16)

    settle(xz.at[pl.ds(0, NZ - 1)], rxz)
    for p in range(NPAIR):
        first = features(xz[lax.rem(z + NPAIR + p, NZ)], False)
        second = features(xz[lax.rem(z + NPAIR - 1 - p, NZ)], False)
        riz[p] = jnp.concatenate([first, second], axis=1).astype(BF16)

    other = {"row_0": y, "row_1": z, "col_0": x, "col_1": 1 - c}

    @pl.loop(0, STEPS)
    def _(i):
        p = i // PER_PAIR
        at = pl.ds(pl.multiple_of(lax.rem(i, PER_PAIR) * CHUNK, CHUNK), CHUNK)
        tile = jnp.exp2(jnp.minimum(fast(ljt[at, :], riz[p]), 0.0))
        high = tile.astype(BF16)
        khi[p, at, :] = high
        klo[p, at, :] = (tile - high.astype(F32)).astype(BF16)
        origin = lax.rem(f + NF - i * NC, NF)

        @pl.when(i > 0)
        def _():
            settle(vf.at[origin], rv.at[i])

        remote(vf.at[origin], vf.at[origin], svf, rvf, other).start()

    settle(vf.at[pl.ds(0, NF // NC)], rvf)

    @pl.loop(0, NF)
    def _(j):
        v = jnp.concatenate([vf[j], jnp.zeros((PAD - VEC, BLK), F32)], axis=0)
        h, m, low = split3(v)
        at = pl.ds(pl.multiple_of(j * BLK, BLK), BLK)
        vcat[0:PAD, at] = h.astype(BF16)
        vcat[PAD : 2 * PAD, at] = m.astype(BF16)
        vcat[2 * PAD : 3 * PAD, at] = low.astype(BF16)

    def block_at(o):
        return pl.ds(pl.multiple_of(o * BLK, BLK), BLK)

    own_vec = vf.at[f]

    @pl.loop(0, NPAIR)
    def _(p):
        a = fast(vcat[...], khi[p])
        b = fast(vcat[0 : 2 * PAD, :], klo[p])
        total = a[0:VEC] + a[PAD : PAD + VEC] + a[2 * PAD : 2 * PAD + VEC] + b[0:VEC] + b[PAD : PAD + VEC]
        total = total * gain
        first, second = lax.rem(z + NPAIR + p, NZ), lax.rem(z + NPAIR - 1 - p, NZ)
        part[:, block_at(first)] = total[:, :BLK]
        part[:, block_at(second)] = total[:, BLK:]
        remote(part.at[:, block_at(first)], pin.at[z], sp, rp, at_z(first)).start()

        @pl.when(p < NPAIR - 1)
        def _():
            remote(part.at[:, block_at(second)], pin.at[z], sp, rp, at_z(second)).start()

    mine = part[:, block_at(z)] + nugget * own_vec[...]
    part[:, block_at(z)] = mine
    pin[z] = mine

    def xc(k):
        o = lax.rem(g + k, NG)
        return o, {"row_0": y, "row_1": z, "col_0": o // NC, "col_1": lax.rem(o, NC)}

    def tile_at(o):
        return pl.ds(pl.multiple_of(o * RHS, RHS), RHS)

    def sum_a(n, value):
        ars[n] = value

        @pl.loop(1, NG)
        def _(k):
            o, device = xc(k)
            remote(ars.at[n, tile_at(o)], ara.at[n, g], sa.at[n], ra.at[n], device).start()

        ara[n, g] = ars[n, tile_at(g)]

    def sum_b(n):
        settle(ara.at[n, pl.ds(0, NG - 1)], ra.at[n])
        arb[n, q] = jnp.sum(ara[n], axis=0)

        @pl.loop(1, NQ)
        def _(k):
            o = lax.rem(q + k, NQ)
            device = {"row_0": o // NZ, "row_1": lax.rem(o, NZ), "col_0": x, "col_1": c}
            remote(arb.at[n, q], arb.at[n, q], sb.at[n], rb.at[n], device).start()

    def sum_c(n):
        settle(arb.at[n, pl.ds(0, NQ - 1)], rb.at[n])
        arc[n, g] = jnp.sum(arb[n], axis=0)

        @pl.loop(1, NG)
        def _(k):
            _, device = xc(k)
            remote(arc.at[n, g], arc.at[n, g], sc.at[n], rc.at[n], device).start()

    def sum_d(n):
        settle(arc.at[n, pl.ds(0, NG - 1)], rc.at[n])
        return arc[n].reshape(RITZ, BLK)

    lane = lax.broadcasted_iota(jnp.int32, (RITZ, BLK), 1)
    settle(wz.at[:, pl.ds(0, (NZ - 1) * BLK)], rw)
    fill = jnp.zeros((BLK - VEC, BLK * NZ), F32)
    coarse_part = matmul(wz[...], jnp.concatenate([part[...], fill], axis=0), ((1,), (1,)))
    ritz_own = own_vec[0:RITZ, :]
    start_own = own_vec[RITZ:VEC, :]
    target_rows = jnp.concatenate(
        [jnp.zeros((RITZ, BLK), F32), tgt[...], jnp.zeros((BLK - VEC, BLK), F32)], axis=0
    )
    coarse_part = jnp.where(lane < RITZ, coarse_part, -coarse_part) + matmul(ritz_own, target_rows, ((1,), (1,)))
    sum_a(0, coarse_part)
    sum_b(0)
    settle(pin.at[pl.ds(0, NZ - 1)], rp)
    image = jnp.sum(pin[...], axis=0)
    zimg = image[0:RITZ]
    r0 = tgt[...] - image[RITZ:VEC]
    both = jnp.concatenate([zimg, r0, jnp.zeros((BLK - VEC, BLK), F32)], axis=0)
    sum_a(1, matmul(zimg, both, ((1,), (1,))))
    sum_c(0)
    sum_b(1)
    first_sum = sum_d(0)
    square = jnp.concatenate([first_sum, jnp.zeros((BLK - RITZ, BLK), F32)], axis=0)
    coarse = 0.5 * (first_sum + square.T[0:RITZ])
    sub = lax.broadcasted_iota(jnp.int32, (RITZ, BLK), 0)
    work = jnp.where(lane < RITZ, jnp.where(lane == sub, 1.0, 0.0), pltpu.roll(coarse, RITZ, 1))

    def eliminate(work, begin, end):
        for k in range(begin, end):
            pivot_row = work[k : k + 1, :] / work[k : k + 1, RITZ + k : RITZ + k + 1]
            column = work[:, RITZ + k : RITZ + k + 1] - jnp.where(sub[:, 0:1] == k, 1.0, 0.0)
            work = work - column * pivot_row
        return work

    work = eliminate(work, 0, 48)
    sum_c(1)
    work = eliminate(work, 48, RITZ)
    inverse = work[:, 0:RITZ]
    amounts = matmul(inverse, first_sum, ((1,), (0,)))
    wide = jnp.concatenate([ritz_own, zimg], axis=1)
    moved = matmul(amounts, wide, ((0,), (0,)))[RITZ:VEC]
    sol = start_own + moved[:, 0:BLK]
    resid = r0 - moved[:, BLK:]
    second_sum = sum_d(1)
    against = second_sum - matmul(second_sum[:, 0:RITZ], amounts, ((1,), (0,)))
    beta = matmul(inverse, against, ((1,), (0,)))
    direction = resid - matmul(beta, ritz_own, ((0,), (0,)))[RITZ:VEC]
    df[f] = direction
    dz[z, 0:RHS] = direction
    dz[z, RHS:] = resid * resid

    @pl.loop(1, NF)
    def _(k):
        remote(df.at[f], df.at[f], sd, rd, xyc(k)).start()

    @pl.loop(1, NZ)
    def _(k):
        remote(dz.at[z], dz.at[z], sdz, rdz, at_z(lax.rem(z + k, NZ))).start()

    settle(df.at[pl.ds(0, NF - 1)], rd)

    @pl.loop(0, NF)
    def _(j):
        h, m, low = split3(df[j])
        dcat[:, block_at(j)] = jnp.concatenate([h, m, low, jnp.zeros_like(h)], axis=0).astype(BF16)

    settle(dz.at[pl.ds(0, NZ - 1)], rdz)

    @pl.loop(0, NPAIR)
    def _(p):
        a = fast(dcat[...], khi[p])
        b = fast(dcat[0:16, :], klo[p])
        total = (a[0:8] + a[8:16] + a[16:24] + b[0:8] + b[8:16]) * gain
        fs[lax.rem(z + NPAIR + p, NZ), 0:RHS] = total[:, :BLK]
        fs[lax.rem(z + NPAIR - 1 - p, NZ), 0:RHS] = total[:, BLK:]

    fs[z, 0:RHS] = fs[z, 0:RHS] + nugget * direction
    curve = jnp.zeros((RHS, BLK), F32)
    square_sum = jnp.zeros((RHS, BLK), F32)
    for o in range(NZ):
        curve = curve + fs[o, 0:RHS] * dz[o, 0:RHS]
        square_sum = square_sum + dz[o, RHS:]
    for o in range(NZ):
        fs[o, RHS:] = curve

    @pl.loop(1, NZ)
    def _(k):
        o = lax.rem(z + k, NZ)
        remote(fs.at[o], fr.at[z], sf, rf, at_z(o)).start()

    fr[z] = fs[z]
    settle(fr.at[pl.ds(0, NZ - 1)], rf)
    arrived = jnp.sum(fr[...], axis=0)
    applied, curve = arrived[0:RHS], arrived[RHS:]
    lanes = lax.broadcasted_iota(jnp.int32, (RHS, BLK), 1)
    curve = curve + pltpu.roll(curve, BLK // 2, 1)
    square_sum = square_sum + pltpu.roll(square_sum, BLK // 2, 1)
    gf[f] = jnp.where(lanes < BLK // 2, curve, square_sum)

    @pl.loop(1, NF)
    def _(k):
        remote(gf.at[f], gf.at[f], sg, rg, xyc(k)).start()

    settle(gf.at[pl.ds(0, NF - 1)], rg)
    both = jnp.sum(gf[...], axis=0)
    bottom = jnp.sum(jnp.where(lanes < BLK // 2, both, 0.0), axis=1, keepdims=True)
    top = jnp.sum(jnp.where(lanes < BLK // 2, 0.0, both), axis=1, keepdims=True)
    step = top / bottom
    out_ref[...] = sol + step * direction
    res_ref[...] = resid - step * applied

    settle(xf.at[pl.ds(0, NF - 1)], sx)
    settle(xz.at[pl.ds(0, NZ - 1)], sxz)
    settle(vf.at[pl.ds(0, NX * NY - 1)], sv)
    settle(vf.at[pl.ds(0, NX * NY)], svf)
    settle(wz.at[:, pl.ds(0, (NZ - 1) * BLK)], sw)
    settle(pin.at[pl.ds(0, NZ - 1)], sp)
    for n in range(2):
        settle(ara.at[n, pl.ds(0, NG - 1)], sa.at[n])
        settle(arb.at[n, pl.ds(0, NQ - 1)], sb.at[n])
        settle(arc.at[n, pl.ds(0, NG - 1)], sc.at[n])
    settle(df.at[pl.ds(0, NF - 1)], sd)
    settle(dz.at[pl.ds(0, NZ - 1)], sdz)
    settle(fr.at[pl.ds(0, NZ - 1)], sf)
    settle(gf.at[pl.ds(0, NF - 1)], sg)


def local(points, inv_scales, amplitude, noise_var, targets, initial, ritz_basis):
    dma = pltpu.SemaphoreType.DMA
    smem = pl.BlockSpec(memory_space=pltpu.SMEM)
    hbm = pl.BlockSpec(memory_space=pl.ANY)
    vmem = pl.BlockSpec(memory_space=pltpu.VMEM)
    return pl.pallas_call(
        body,
        out_shape=(jax.ShapeDtypeStruct((RHS, BLK), F32), jax.ShapeDtypeStruct((RHS, BLK), F32)),
        in_specs=[smem, smem, smem, hbm, hbm, hbm, hbm],
        out_specs=(vmem, vmem),
        scratch_shapes=[
            pltpu.VMEM((FEAT, BLK), F32),
            pltpu.VMEM((NF, FEAT, BLK), F32),
            pltpu.VMEM((NZ, FEAT, BLK), F32),
            pltpu.VMEM((NF, VEC, BLK), F32),
            pltpu.VMEM((RITZ, NZ * BLK), F32),
            pltpu.VMEM((RHS, BLK), F32),
            pltpu.VMEM((NJ, BLK), BF16),
            pltpu.VMEM((NPAIR, BLK, 2 * BLK), BF16),
            pltpu.VMEM((NPAIR, NJ, 2 * BLK), BF16),
            pltpu.VMEM((NPAIR, NJ, 2 * BLK), BF16),
            pltpu.VMEM((3 * PAD, NJ), BF16),
            pltpu.VMEM((VEC, NZ * BLK), F32),
            pltpu.VMEM((NZ, VEC, BLK), F32),
            pltpu.VMEM((2, RITZ, BLK), F32),
            pltpu.VMEM((2, NG, RHS, BLK), F32),
            pltpu.VMEM((2, NQ, RHS, BLK), F32),
            pltpu.VMEM((2, NG, RHS, BLK), F32),
            pltpu.VMEM((NF, RHS, BLK), F32),
            pltpu.VMEM((NZ, 2 * RHS, BLK), F32),
            pltpu.VMEM((NZ, 2 * RHS, BLK), F32),
            pltpu.VMEM((NZ, 2 * RHS, BLK), F32),
            pltpu.VMEM((NF, RHS, BLK), F32),
            pltpu.VMEM((4 * RHS, NJ), BF16),
            dma((5,)), dma, dma, dma((NX * NY,)), dma, dma, dma, dma((2,)), dma((2,)), dma((2,)), dma, dma, dma, dma,
            dma, dma, dma, dma, dma, dma, dma((2,)), dma((2,)), dma((2,)), dma, dma, dma, dma,
        ],
        compiler_params=pltpu.CompilerParams(
            collective_id=0, has_side_effects=True, vmem_limit_bytes=60 * 1024 * 1024
        ),
    )(amplitude, noise_var, inv_scales, points, targets, initial, ritz_basis)


def solution(mesh):
    torus = Mesh(mesh.devices.reshape(NY, NZ, NX, NC), ("row_0", "row_1", "col_0", "col_1"))
    split = P(None, ("col_0", "col_1", "row_0", "row_1"))
    return jax.shard_map(
        local,
        mesh=torus,
        in_specs=(split, P(), P(), P(), split, split, split),
        out_specs=(split, split),
        check_vma=False,
    )
```

time: 257 us -> 84.5 us (0.33)
  blocking collectives: 110 us -> 0 us
  Pallas kernels: 0 us -> 80.6 us
  matrix products: 54.8 us -> 0 us
  waiting for transfers between devices: 38.5 us -> 0 us
  starting transfers between devices: 23.5 us -> 0 us
  other arithmetic: 15.1 us -> 0 us
  local copies, waits for them, and re-layouts: 11.3 us -> 1.86 us
    all_to_all x9 -> x0, blocking collectives: 110 us -> none  [the longest x8 98.2 us: from_everyone(): return lax.all_to_all(copies, axis, split_axis=0, concat_axis=0, tiled=True)]
    pallas_call x0 -> x1, Pallas kernels: none -> 80.6 us  [local(): pl.pallas_call(body, out_shape=(jax.ShapeDtypeStruct((RHS, BLK), F32), ja...]
    dot_general x11 -> x0, matrix products: 54.4 us -> none  [the longest x10 35.7 us: matmul(): jnp.dot(left, right, precision=HIGH, preferred_element_type=jnp.float32)]
    all_to_all x3 -> x0, waiting for transfers between devices: 38.5 us -> none  [the longest x1 27 us: sum_at_owner(): lax.all_to_all(pieces, axis, split_axis=0, concat_axis=0, tiled=True)]
    all_to_all x3 -> x0, starting transfers between devices: 23.5 us -> none  [the longest x2 17 us: from_everyone(): return lax.all_to_all(copies, axis, split_axis=0, concat_axis=0, tiled=True)]
    another operation x5 -> x0, other arithmetic: 12.1 us -> none  [the longest x3 6.52 us: local(): factor = jnp.linalg.cholesky(coarse)]
    unnamed x9 -> x4, local copies, waits for them, and re-layouts: 6.39 us -> 1.86 us
    broadcast_in_dim x10 -> x0, local copies, waits for them, and re-layouts: 3.21 us -> none  [from_everyone(): copies = jnp.broadcast_to(array, (lax.axis_size(axis), *array.shape))]
  transfers between devices with their start and end apart: 3 -> 0, of which waited for: 3 -> 0; matrix products, arithmetic and copies ran while one was open for 1% -> 0% of each run, Pallas kernels for 0% -> 0%
where the time goes in v1:
time: 84.5 us; the launch traced here: 84.4 us
  Pallas kernels  80.6 us (95%)
  between operations  1.94 us (2%)
  local copies, waits for them, and re-layouts  1.86 us (2%)
    pallas_call x1, Pallas kernels, local(): pl.pallas_call(body, out_shape=(jax.ShapeDtypeStruct((RHS, BLK), F32), ja...  80.6 us
    unnamed x4, local copies, waits for them, and re-layouts  1.86 us

profile of v1, /device:TPU:1, one launch (start us, length us, event | category | flops | bytes accessed | tf_op | source)
XLA Modules:
  0.0 84.4 jit_solution(15432481875798384555)
XLA Ops:
  1.9 80.6 %shard_map.86 = (f32[8,128]{1,0:T(8,128)}, f32[8,128]{1,0:T(8,128)}) custom-call(f32[1]{0:T(128)S(6)} %copy.11.gain_ref, f32[1]{0:T(128)S(6)} %copy.12.nugget_ref, f32[16]{0:T(128)} %scales_ref.1, f32[16,128]{1,0:T(8,128)} %points_ref.1, f32[8,128]{1,0:T(8,128)} %targets_ref.1, f32[8,128]{1,0:T(8,128)} %initial_ref.1, f32[64,128]{1,0:T(8,128)} %ritz_ref.1), custom_call_target="tpu_custom_call" | custom-call | tf_op jit(solution)/shard_map/pallas_call | solution.py:380
  82.5 0.0 copy-start
  82.5 1.3 %copy.13 = f32[8,128]{1,0:T(8,128)} copy(f32[8,128]{1,0:T(8,128)} %get-tuple-element.4) | data formatting | bytes 8192
  83.8 0.0 copy-done
  83.8 0.6 copy.14
Async XLA Ops:
  82.5 1.3 %copy-start = (f32[8,128]{1,0:T(8,128)S(1)}, f32[8,128]{1,0:T(8,128)}, u32[]{:S(2)}) copy-start(f32[8,128]{1,0:T(8,128)} %get-tuple-element.5) | copy-start | bytes 12292

commit v2 on v1

v2 whole, which is shorter than its diff:
```python
import functools
import math

import jax
import jax.numpy as jnp
from jax import lax
from jax.experimental import pallas as pl
from jax.experimental.pallas import tpu as pltpu
from jax.sharding import Mesh
from jax.sharding import PartitionSpec as P

F32 = jnp.float32
BF16 = jnp.bfloat16
HIGH = lax.Precision.HIGHEST
MESH = pl.DeviceIdType.MESH
NY, NZ, NX, NC = 4, 8, 4, 2
NF = NX * NY * NC
NG = NX * NC
NQ = NY * NZ
BLK = 128
FEAT = 16
RITZ = 64
RHS = 8
VEC = RITZ + RHS
PAD = 80
NJ = NF * BLK
CHIPS = NX * NY
HALF = CHIPS * BLK
ROWS = 1024
HOLD = False
NI = NZ * BLK
NEAR = (0, 1, 3, 2)
LOG2E = 1.4426950408889634


def split3(a):
    high = a.astype(BF16).astype(F32)
    rest = a - high
    mid = rest.astype(BF16).astype(F32)
    low = (rest - mid).astype(BF16).astype(F32)
    return high, mid, low


def matmul(a, b, dims):
    return lax.dot_general(a, b, (dims, ((), ())), precision=HIGH, preferred_element_type=F32)


def fast(a, b):
    return jnp.dot(a, b, preferred_element_type=F32)


def features(y, left):
    h, m, low = split3(y)
    sh, sm, sl = split3(-0.5 * jnp.sum(y * y, axis=0, keepdims=True))
    row = lax.broadcasted_iota(jnp.int32, (FEAT, BLK), 0)
    at = 0 if left else 3
    ones = (row < 6) & ((row >= 3) if left else (row < 3))
    extra = jnp.where(row == at, sh, jnp.where(row == at + 1, sm, jnp.where(row == at + 2, sl, 0.0)))
    extra = jnp.where(ones, 1.0, extra)
    zero = jnp.zeros((FEAT, BLK), F32)
    parts = [h, m, h, low, h, m, extra, zero] if left else [h, h, m, h, low, m, extra, zero]
    return jnp.concatenate(parts, axis=0)


def inverse2(m):
    a, b, e, d = m
    r = 1.0 / (a * d - b * e)
    return d * r, -b * r, -e * r, a * r


def multiply2(m, n):
    return (
        m[0] * n[0] + m[1] * n[2],
        m[0] * n[1] + m[1] * n[3],
        m[2] * n[0] + m[3] * n[2],
        m[2] * n[1] + m[3] * n[3],
    )


def eliminate(work):
    def full(a):
        return jnp.broadcast_to(a, (RHS, BLK))

    sub = lax.broadcasted_iota(jnp.int32, (RHS, BLK), 0)
    tiles = [work[RHS * i : RHS * (i + 1)] for i in range(RITZ // RHS)]
    for k in range(0, RITZ, 4):
        v, r = k // RHS, k % RHS
        cols = [[full(t[:, RITZ + k + j : RITZ + k + j + 1]) for t in tiles] for j in range(4)]
        u = [full(tiles[v][r + i : r + i + 1]) for i in range(4)]
        m = [[full(cols[j][v][r + i : r + i + 1]) for j in range(4)] for i in range(4)]
        b = (m[0][2], m[0][3], m[1][2], m[1][3])
        first = inverse2((m[0][0], m[0][1], m[1][0], m[1][1]))
        low = multiply2((m[2][0], m[2][1], m[3][0], m[3][1]), first)
        schur = tuple(p - q for p, q in zip((m[2][2], m[2][3], m[3][2], m[3][3]), multiply2(low, b)))
        second = inverse2(schur)
        t2 = u[2] - low[0] * u[0] - low[1] * u[1]
        t3 = u[3] - low[2] * u[0] - low[3] * u[1]
        n2 = second[0] * t2 + second[1] * t3
        n3 = second[2] * t2 + second[3] * t3
        t0 = u[0] - b[0] * n2 - b[1] * n3
        t1 = u[1] - b[2] * n2 - b[3] * n3
        n0 = first[0] * t0 + first[1] * t1
        n1 = first[2] * t0 + first[3] * t1
        for j in range(4):
            cols[j][v] = jnp.where(sub == r + j, cols[j][v] - 1.0, cols[j][v])
        tiles = [
            t - (cols[0][i] * n0 + cols[1][i] * n1) - (cols[2][i] * n2 + cols[3][i] * n3)
            for i, t in enumerate(tiles)
        ]
    return jnp.concatenate(tiles, axis=0)


def body(
    gain_ref, nugget_ref, scales_ref, points_ref, targets_ref, initial_ref, ritz_ref, out_ref, res_ref,
    px, xf, xz, vf, wz, tgt, ljt, riz, khi, klo, vcat, part, pin, ars, ara, arb, arc, rf, rz, tz, tf, acc, fs, fr, gf,
    sem_in, rx, rxf, rxz, rv, rvf, rw, rp, ra, rb, rc, rr, rrz, rtz, rt, rs, rg,
    sx, sxf, sxz, sv, svf, sw, sp, sa, sb, sc, sr, srz, stz, st, ss, sg,
):
    y = lax.axis_index("row_0")
    z = lax.axis_index("row_1")
    x = lax.axis_index("col_0")
    c = lax.axis_index("col_1")
    f = (x * NY + y) * NC + c
    g = x * NC + c
    q = y * NZ + z
    xs = [lax.rem(x + k, NX) for k in range(NX)]
    ys = [lax.rem(y + k, NY) for k in range(NY)]
    zs = [lax.rem(z + k, NZ) for k in range(NZ)]
    other = {"row_0": y, "row_1": z, "col_0": x, "col_1": 1 - c}
    along_z = [(zs[k], {"row_0": y, "row_1": zs[k], "col_0": x, "col_1": c}) for k in (4, 3, 5, 2, 6, 1, 7)]

    def chip(k):
        return {"row_0": ys[NEAR[k % NY]], "row_1": z, "col_0": xs[NEAR[k // NY]]}

    plane = [(k, o, {**chip(k), "col_1": 1 - c if o else c}) for k in range(CHIPS) for o in (0, 1) if k or o]
    same_core = [(k, device) for k, o, device in plane if not o]
    row_group = [
        {"row_0": ys[a], "row_1": zs[b], "col_0": x, "col_1": c}
        for b in (4, 3, 5, 2, 6, 1, 7, 0)
        for a in (2, 1, 3, 0)
        if a or b
    ]
    column_group = [(g + 1 - 2 * c, other)] + [
        (xs[a] * NC + o, {"row_0": y, "row_1": z, "col_0": xs[a], "col_1": o}) for a in (2, 1, 3) for o in range(NC)
    ]

    def send(src, dst, sent, arrived, device):
        pltpu.make_async_remote_copy(
            src_ref=src, dst_ref=dst, send_sem=sent, recv_sem=arrived, device_id=device, device_id_type=MESH
        ).start()

    def settle(ref, sem):
        pltpu.make_async_copy(ref, ref, sem).wait()

    def block_at(o):
        return pl.ds(pl.multiple_of(o * BLK, BLK), BLK)

    loads = [
        pltpu.make_async_copy(points_ref, px, sem_in.at[0]),
        pltpu.make_async_copy(ritz_ref, vf.at[0, 0, pl.ds(0, RITZ)], sem_in.at[1]),
        pltpu.make_async_copy(initial_ref, vf.at[0, 0, pl.ds(RITZ, RHS)], sem_in.at[2]),
        pltpu.make_async_copy(targets_ref, tgt, sem_in.at[3]),
        pltpu.make_async_copy(ritz_ref, wz.at[:, block_at(z)], sem_in.at[4]),
    ]
    for load in loads:
        load.start()
    barrier = pltpu.get_barrier_semaphore()
    for device in [d for _, d in along_z] + [d for _, _, d in plane[::-1]]:
        pl.semaphore_signal(barrier, inc=1, device_id=device, device_id_type=MESH)

    gain = gain_ref[0]
    nugget = nugget_ref[0]
    row = lax.broadcasted_iota(jnp.int32, (FEAT, BLK), 0)
    scale = jnp.zeros((FEAT, BLK), F32)
    for i in range(FEAT):
        scale = jnp.where(row == i, scales_ref[i], scale)
    loads[0].wait()
    scaled = px[...] * scale * math.sqrt(LOG2E)
    xf[0, 0] = scaled
    xz[z] = scaled
    for load in loads[1:]:
        load.wait()
    pl.semaphore_wait(barrier, NF - 1 + NZ - 1)

    for _, device in along_z:
        send(xz.at[z], xz.at[z], sxz, rxz, device)
    for k, device in same_core:
        send(xf.at[0, 0], xf.at[0, k], sx, rx, device)
    own_vec = vf.at[0, 0]
    own_w = wz.at[:, block_at(z)]

    def bulk():
        for k, device in same_core:
            send(own_vec, vf.at[0, k], sv, rv, device)
        for _, device in along_z:
            send(own_w, own_w, sw, rw, device)

    if not HOLD:
        bulk()
    settle(xf.at[0, pl.ds(0, CHIPS - 1)], rx)
    send(xf.at[0], xf.at[1], sxf, rxf, other)
    if HOLD:
        bulk()

    def side(h):
        for k in range(CHIPS):
            at = (h * CHIPS + k) * BLK
            ljt[at : at + BLK, :] = features(xf[h, k], True).T.astype(BF16)

    def tile_rows(h):
        @pl.loop(h * HALF // ROWS, (h + 1) * HALF // ROWS)
        def _(i):
            at = pl.ds(pl.multiple_of(i * ROWS, ROWS), ROWS)
            tile = jnp.exp2(jnp.minimum(fast(ljt[at, :], riz[...]), 0.0))
            high = tile.astype(BF16)
            khi[at, :] = high
            klo[at, :] = (tile - high.astype(F32)).astype(BF16)

    side(0)
    settle(xz.at[pl.ds(0, NZ - 1)], rxz)
    for o in range(NZ):
        riz[:, o * BLK : (o + 1) * BLK] = features(xz[o], False).astype(BF16)
    tile_rows(0)
    settle(xf.at[1], rxf)
    side(1)
    tile_rows(1)

    def vectors(h):
        for k in range(CHIPS):
            v = jnp.concatenate([vf[h, k], jnp.zeros((PAD - VEC, BLK), F32)], axis=0)
            at = (h * CHIPS + k) * BLK
            vcat[:, at : at + BLK] = jnp.concatenate(split3(v), axis=0).astype(BF16)

    def product(h):
        at = pl.ds(h * HALF, HALF)

        @pl.loop(0, NI // (2 * BLK))
        def _(p):
            to = pl.ds(pl.multiple_of(p * 2 * BLK, 2 * BLK), 2 * BLK)
            a = fast(vcat[:, at], khi[at, to])
            b = fast(vcat[0 : 2 * PAD, at], klo[at, to])
            total = a[0:VEC] + a[PAD : PAD + VEC] + a[2 * PAD : 2 * PAD + VEC] + b[0:VEC] + b[PAD : PAD + VEC]
            part[:, to] = total if h == 0 else (part[:, to] + total) * gain

    settle(vf.at[0, pl.ds(0, CHIPS - 1)], rv)
    send(vf.at[0], vf.at[1], svf, rvf, other)
    vectors(0)
    product(0)
    settle(vf.at[1], rvf)
    vectors(1)
    product(1)

    mine = part[:, block_at(z)] + nugget * own_vec[...]
    part[:, block_at(z)] = mine
    pin[z] = mine

    lane = lax.broadcasted_iota(jnp.int32, (RITZ, BLK), 1)
    settle(wz.at[:, pl.ds(0, (NZ - 1) * BLK)], rw)
    fill = jnp.zeros((BLK - VEC, NI), F32)
    coarse_part = matmul(wz[...], jnp.concatenate([part[...], fill], axis=0), ((1,), (1,)))
    ritz_own = own_vec[0:RITZ, :]
    start_own = own_vec[RITZ:VEC, :]
    target_rows = jnp.concatenate([jnp.zeros((RITZ, BLK), F32), tgt[...], jnp.zeros((BLK - VEC, BLK), F32)], axis=0)
    coarse_part = jnp.where(lane < RITZ, coarse_part, -coarse_part) + matmul(ritz_own, target_rows, ((1,), (1,)))
    ars[...] = coarse_part.reshape(NG, RHS, BLK)
    for o, device in column_group:
        send(ars.at[o], ara.at[g], sa, ra, device)
    ara[g] = ars[g]
    settle(ara.at[pl.ds(0, NG - 1)], ra)
    arb[q] = jnp.sum(ara[...], axis=0)
    for device in row_group:
        send(arb.at[q], arb.at[q], sb, rb, device)
    for o, device in along_z:
        send(part.at[:, block_at(o)], pin.at[z], sp, rp, device)
    settle(arb.at[pl.ds(0, NQ - 1)], rb)
    arc[g] = jnp.sum(arb[...], axis=0)
    for _, device in column_group:
        send(arc.at[g], arc.at[g], sc, rc, device)
    settle(arc.at[pl.ds(0, NG - 1)], rc)
    first_sum = arc[...].reshape(RITZ, BLK)
    square = jnp.concatenate([first_sum, jnp.zeros((BLK - RITZ, BLK), F32)], axis=0)
    coarse = 0.5 * (first_sum + square.T[0:RITZ])
    sub = lax.broadcasted_iota(jnp.int32, (RITZ, BLK), 0)
    work = jnp.where(lane < RITZ, jnp.where(lane == sub, 1.0, 0.0), pltpu.roll(coarse, RITZ, 1))
    work = eliminate(work)
    inverse = work[:, 0:RITZ]
    amounts = matmul(inverse, first_sum, ((1,), (0,)))
    settle(pin.at[pl.ds(0, NZ - 1)], rp)
    image = jnp.sum(pin[...], axis=0)
    zimg = image[0:RITZ]
    r0 = tgt[...] - image[RITZ:VEC]
    wide = jnp.concatenate([ritz_own, zimg], axis=1)
    moved = matmul(amounts, wide, ((0,), (0,)))[RITZ:VEC]
    resid = r0 - moved[:, BLK:]
    rf[0, 0] = resid
    rz[z] = resid

    for k, o, device in plane[::-1]:
        send(rf.at[0, 0], rf.at[o, k], sr, rr.at[o], device)
    for _, device in along_z:
        send(rz.at[z], rz.at[z], srz, rrz, device)
    sol = start_own + moved[:, 0:BLK]
    lanes = lax.broadcasted_iota(jnp.int32, (RHS, BLK), 1)
    tall = jnp.concatenate([zimg, jnp.zeros((BLK - RITZ, BLK), F32)], axis=0)
    against = matmul(resid, tall, ((1,), (1,)))
    norm = jnp.sum(resid * resid, axis=1, keepdims=True)
    tz[z] = jnp.where(lanes < RITZ, against, jnp.where(lanes == RITZ, norm, 0.0))
    for _, device in along_z:
        send(tz.at[z], tz.at[z], stz, rtz, device)

    def second(h):
        h_, m, low = split3(jnp.concatenate([rf[h, k] for k in range(CHIPS)], axis=1))
        v = jnp.concatenate([h_, m, low, jnp.zeros_like(h_)], axis=0).astype(BF16)
        at = pl.ds(h * HALF, HALF)
        a = fast(v, khi[at, :])
        b = fast(v[0:16], klo[at, :])
        return a[0:8] + a[8:16] + a[16:24] + b[0:8] + b[8:16]

    settle(rf.at[0, pl.ds(0, CHIPS - 1)], rr.at[0])
    acc[...] = second(0)
    settle(rf.at[1], rr.at[1])
    acc[...] = (acc[...] + second(1)) * gain
    settle(rz.at[pl.ds(0, NZ - 1)], rrz)
    acc[:, block_at(z)] = acc[:, block_at(z)] + nugget * resid
    curve = jnp.zeros((RHS, BLK), F32)
    for o in range(NZ):
        curve = curve + acc[:, o * BLK : (o + 1) * BLK] * rz[o]
    for o in range(NZ):
        fs[o, 0:RHS] = acc[:, o * BLK : (o + 1) * BLK]
        fs[o, RHS:] = curve
    for o, device in along_z:
        send(fs.at[o], fr.at[z], ss, rs, device)
    fr[z] = fs[z]
    settle(tz.at[pl.ds(0, NZ - 1)], rtz)
    tf[f] = jnp.sum(tz[...], axis=0)
    for _, _, device in plane[::-1]:
        send(tf.at[f], tf.at[f], st, rt, device)
    settle(fr.at[pl.ds(0, NZ - 1)], rs)
    arrived = jnp.sum(fr[...], axis=0)
    applied, curve = arrived[0:RHS], arrived[RHS:]
    gf[f] = curve
    for _, _, device in plane[::-1]:
        send(gf.at[f], gf.at[f], sg, rg, device)
    settle(tf.at[pl.ds(0, NF - 1)], rt)
    stats = jnp.sum(tf[...], axis=0)
    beta = matmul(stats[:, 0:RITZ], inverse, ((1,), (0,)))
    shift = matmul(beta, wide, ((1,), (0,)))
    direction = resid - shift[:, 0:BLK]
    applied = applied - shift[:, BLK:]
    deflated = jnp.sum(stats[:, 0:RITZ] * beta, axis=1, keepdims=True)
    settle(gf.at[pl.ds(0, NF - 1)], rg)
    curve = jnp.sum(jnp.sum(gf[...], axis=0), axis=1, keepdims=True) - deflated
    step = stats[:, RITZ : RITZ + 1] / curve
    out_ref[...] = sol + step * direction
    res_ref[...] = resid - step * applied

    settle(xf.at[0, pl.ds(0, CHIPS - 1)], sx)
    settle(xf.at[0], sxf)
    settle(xz.at[pl.ds(0, NZ - 1)], sxz)
    settle(vf.at[0, pl.ds(0, CHIPS - 1)], sv)
    settle(vf.at[0], svf)
    settle(wz.at[:, pl.ds(0, (NZ - 1) * BLK)], sw)
    settle(pin.at[pl.ds(0, NZ - 1)], sp)
    settle(ara.at[pl.ds(0, NG - 1)], sa)
    settle(arb.at[pl.ds(0, NQ - 1)], sb)
    settle(arc.at[pl.ds(0, NG - 1)], sc)
    settle(rf.at[0, pl.ds(0, CHIPS - 1)], sr)
    settle(rf.at[1], sr)
    settle(rz.at[pl.ds(0, NZ - 1)], srz)
    settle(tz.at[pl.ds(0, NZ - 1)], stz)
    settle(tf.at[pl.ds(0, NF - 1)], st)
    settle(fr.at[pl.ds(0, NZ - 1)], ss)
    settle(gf.at[pl.ds(0, NF - 1)], sg)


def local(points, inv_scales, amplitude, noise_var, targets, initial, ritz_basis):
    dma = pltpu.SemaphoreType.DMA
    smem = pl.BlockSpec(memory_space=pltpu.SMEM)
    hbm = pl.BlockSpec(memory_space=pl.ANY)
    vmem = pl.BlockSpec(memory_space=pltpu.VMEM)
    return pl.pallas_call(
        body,
        out_shape=(jax.ShapeDtypeStruct((RHS, BLK), F32), jax.ShapeDtypeStruct((RHS, BLK), F32)),
        in_specs=[smem, smem, smem, hbm, hbm, hbm, hbm],
        out_specs=(vmem, vmem),
        scratch_shapes=[
            pltpu.VMEM((FEAT, BLK), F32),
            pltpu.VMEM((NC, CHIPS, FEAT, BLK), F32),
            pltpu.VMEM((NZ, FEAT, BLK), F32),
            pltpu.VMEM((NC, CHIPS, VEC, BLK), F32),
            pltpu.VMEM((RITZ, NI), F32),
            pltpu.VMEM((RHS, BLK), F32),
            pltpu.VMEM((NJ, BLK), BF16),
            pltpu.VMEM((BLK, NI), BF16),
            pltpu.VMEM((NJ, NI), BF16),
            pltpu.VMEM((NJ, NI), BF16),
            pltpu.VMEM((3 * PAD, NJ), BF16),
            pltpu.VMEM((VEC, NI), F32),
            pltpu.VMEM((NZ, VEC, BLK), F32),
            pltpu.VMEM((NG, RHS, BLK), F32),
            pltpu.VMEM((NG, RHS, BLK), F32),
            pltpu.VMEM((NQ, RHS, BLK), F32),
            pltpu.VMEM((NG, RHS, BLK), F32),
            pltpu.VMEM((NC, CHIPS, RHS, BLK), F32),
            pltpu.VMEM((NZ, RHS, BLK), F32),
            pltpu.VMEM((NZ, RHS, BLK), F32),
            pltpu.VMEM((NF, RHS, BLK), F32),
            pltpu.VMEM((RHS, NI), F32),
            pltpu.VMEM((NZ, 2 * RHS, BLK), F32),
            pltpu.VMEM((NZ, 2 * RHS, BLK), F32),
            pltpu.VMEM((NF, RHS, BLK), F32),
            dma((5,)), dma, dma, dma, dma, dma, dma, dma, dma, dma, dma, dma((NC,)), dma, dma, dma, dma, dma,
            dma, dma, dma, dma, dma, dma, dma, dma, dma, dma, dma, dma, dma, dma, dma, dma,
        ],
        compiler_params=pltpu.CompilerParams(
            collective_id=0, has_side_effects=True, vmem_limit_bytes=60 * 1024 * 1024
        ),
    )(amplitude, noise_var, inv_scales, points, targets, initial, ritz_basis)


def solution(mesh):
    torus = Mesh(mesh.devices.reshape(NY, NZ, NX, NC), ("row_0", "row_1", "col_0", "col_1"))
    split = P(None, ("col_0", "col_1", "row_0", "row_1"))
    return jax.shard_map(
        local,
        mesh=torus,
        in_specs=(split, P(), P(), P(), split, split, split),
        out_specs=(split, split),
        check_vma=False,
    )
```

time: 84.5 us -> 69.7 us (0.82)
  Pallas kernels: 80.6 us -> 65.7 us
    pallas_call x1, Pallas kernels: 80.6 us -> 65.7 us  [local(): pl.pallas_call(body, out_shape=(jax.ShapeDtypeStruct((RHS, BLK), F32), ja...]
where the time goes in v2:
time: 69.7 us; the launch traced here: 69.5 us
  Pallas kernels  65.7 us (94%)
  between operations  1.94 us (3%)
  local copies, waits for them, and re-layouts  1.86 us (3%)
    pallas_call x1, Pallas kernels, local(): pl.pallas_call(body, out_shape=(jax.ShapeDtypeStruct((RHS, BLK), F32), ja...  65.7 us
    unnamed x4, local copies, waits for them, and re-layouts  1.86 us

profile of v2, /device:TPU:1, one launch (start us, length us, event | category | flops | bytes accessed | tf_op | source)
XLA Modules:
  0.0 69.5 jit_solution(15827603575262780836)
XLA Ops:
  1.9 65.7 %shard_map.86 = (f32[8,128]{1,0:T(8,128)}, f32[8,128]{1,0:T(8,128)}) custom-call(f32[1]{0:T(128)S(6)} %copy.11.gain_ref, f32[1]{0:T(128)S(6)} %copy.12.nugget_ref, f32[16]{0:T(128)} %scales_ref.1, f32[16,128]{1,0:T(8,128)} %points_ref.1, f32[8,128]{1,0:T(8,128)} %targets_ref.1, f32[8,128]{1,0:T(8,128)} %initial_ref.1, f32[64,128]{1,0:T(8,128)} %ritz_ref.1), custom_call_target="tpu_custom_call" | custom-call | tf_op jit(solution)/shard_map/pallas_call | solution.py:381
  67.6 0.0 copy-start
  67.7 1.3 %copy.13 = f32[8,128]{1,0:T(8,128)} copy(f32[8,128]{1,0:T(8,128)} %get-tuple-element.4) | data formatting | bytes 8192
  68.9 0.0 copy-done
  68.9 0.6 copy.14
Async XLA Ops:
  67.6 1.3 %copy-start = (f32[8,128]{1,0:T(8,128)S(1)}, f32[8,128]{1,0:T(8,128)}, u32[]{:S(2)}) copy-start(f32[8,128]{1,0:T(8,128)} %get-tuple-element.5) | copy-start | bytes 12292

commit v3 on v2

v3 whole, which is shorter than its diff:
```python
import functools
import math

import jax
import jax.numpy as jnp
from jax import lax
from jax.experimental import pallas as pl
from jax.experimental.pallas import tpu as pltpu
from jax.sharding import Mesh
from jax.sharding import PartitionSpec as P

F32 = jnp.float32
BF16 = jnp.bfloat16
HIGH = lax.Precision.HIGHEST
MESH = pl.DeviceIdType.MESH
NY, NZ, NX, NC = 4, 8, 4, 2
CHIPS = NX * NY
NF = CHIPS * NC
BLK = 128
FEAT = 16
RITZ = 64
RHS = 8
VEC = RITZ + RHS
PAD = 80
NJ = NF * BLK
HALF = CHIPS * BLK
ROWS = 1024
NI = NZ * BLK
NEAR = sorted(((a, b) for a in range(NX) for b in range(NY)), key=lambda o: (min(o[0], NX - o[0]) + min(o[1], NY - o[1]), o))
HERE = CHIPS // 2
FAR = (4, 3, 5, 2, 6, 1, 7, 0)
OWN = NZ - 1
LOG2E = 1.4426950408889634


def split3(a):
    high = a.astype(BF16).astype(F32)
    rest = a - high
    mid = rest.astype(BF16).astype(F32)
    low = (rest - mid).astype(BF16).astype(F32)
    return high, mid, low


def matmul(a, b, dims):
    return lax.dot_general(a, b, (dims, ((), ())), precision=HIGH, preferred_element_type=F32)


def fast(a, b):
    return jnp.dot(a, b, preferred_element_type=F32)


def features(y, left):
    h, m, low = split3(y)
    sh, sm, sl = split3(-0.5 * jnp.sum(y * y, axis=0, keepdims=True))
    row = lax.broadcasted_iota(jnp.int32, (FEAT, BLK), 0)
    at = 0 if left else 3
    ones = (row < 6) & ((row >= 3) if left else (row < 3))
    extra = jnp.where(row == at, sh, jnp.where(row == at + 1, sm, jnp.where(row == at + 2, sl, 0.0)))
    extra = jnp.where(ones, 1.0, extra)
    zero = jnp.zeros((FEAT, BLK), F32)
    parts = [h, m, h, low, h, m, extra, zero] if left else [h, h, m, h, low, m, extra, zero]
    return jnp.concatenate(parts, axis=0)


def inverse2(m):
    a, b, e, d = m
    r = 1.0 / (a * d - b * e)
    return d * r, -b * r, -e * r, a * r


def multiply2(m, n):
    return (
        m[0] * n[0] + m[1] * n[2],
        m[0] * n[1] + m[1] * n[3],
        m[2] * n[0] + m[3] * n[2],
        m[2] * n[1] + m[3] * n[3],
    )


def eliminate(work):
    def full(a):
        return jnp.broadcast_to(a, (RHS, BLK))

    sub = lax.broadcasted_iota(jnp.int32, (RHS, BLK), 0)
    tiles = [work[RHS * i : RHS * (i + 1)] for i in range(RITZ // RHS)]
    for k in range(0, RITZ, 4):
        v, r = k // RHS, k % RHS
        cols = [[full(t[:, RITZ + k + j : RITZ + k + j + 1]) for t in tiles] for j in range(4)]
        u = [full(tiles[v][r + i : r + i + 1]) for i in range(4)]
        m = [[full(cols[j][v][r + i : r + i + 1]) for j in range(4)] for i in range(4)]
        b = (m[0][2], m[0][3], m[1][2], m[1][3])
        first = inverse2((m[0][0], m[0][1], m[1][0], m[1][1]))
        low = multiply2((m[2][0], m[2][1], m[3][0], m[3][1]), first)
        schur = tuple(p - q for p, q in zip((m[2][2], m[2][3], m[3][2], m[3][3]), multiply2(low, b)))
        second = inverse2(schur)
        t2 = u[2] - low[0] * u[0] - low[1] * u[1]
        t3 = u[3] - low[2] * u[0] - low[3] * u[1]
        n2 = second[0] * t2 + second[1] * t3
        n3 = second[2] * t2 + second[3] * t3
        t0 = u[0] - b[0] * n2 - b[1] * n3
        t1 = u[1] - b[2] * n2 - b[3] * n3
        n0 = first[0] * t0 + first[1] * t1
        n1 = first[2] * t0 + first[3] * t1
        for j in range(4):
            cols[j][v] = jnp.where(sub == r + j, cols[j][v] - 1.0, cols[j][v])
        tiles = [
            t - (cols[0][i] * n0 + cols[1][i] * n1) - (cols[2][i] * n2 + cols[3][i] * n3)
            for i, t in enumerate(tiles)
        ]
    return jnp.concatenate(tiles, axis=0)


def body(
    gain_ref, nugget_ref, scales_ref, points_ref, targets_ref, initial_ref, ritz_ref, out_ref,
    gain_at, nugget_at, scales_at, px, xf, xz, vf, wz, tgt, ljt, riz, khi, klo, vcat, part, pin, ars, ara, arb, arc, rf, rz, tz, tf, acc, fr, gf, hz,
    sem_in, rx, rxf, rxz, rv, rvf, rw, rp, ra, rb, rc, rr, rrz, rtz, rt, rs, rg, rh,
    sx, sxf, sxz, sv, svf, sw, sp, sa, sb, sc, sr, srz, stz, st, ss, sg, sh,
):
    y = lax.axis_index("row_0")
    z = lax.axis_index("row_1")
    x = lax.axis_index("col_0")
    c = lax.axis_index("col_1")
    f = (x * NY + y) * NC + c
    xs = [lax.rem(x + k, NX) for k in range(NX)]
    ys = [lax.rem(y + k, NY) for k in range(NY)]
    zs = [lax.rem(z + k, NZ) for k in range(NZ)]
    other = {"row_0": y, "row_1": z, "col_0": x, "col_1": 1 - c}
    along_z = [
        (FAR.index((NZ - k) % NZ), i, {"row_0": y, "row_1": zs[k], "col_0": x, "col_1": c}) for i, k in enumerate(FAR[:-1])
    ]

    def chip(k):
        return {"row_0": ys[NEAR[k][1]], "row_1": z, "col_0": xs[NEAR[k][0]]}

    plane = [(k, o, {**chip(k), "col_1": 1 - c if o else c}) for k in range(CHIPS) for o in (0, 1) if k or o]
    same_core = [(k, device) for k, o, device in plane if not o]
    def send(src, dst, sent, arrived, device):
        pltpu.make_async_remote_copy(
            src_ref=src, dst_ref=dst, send_sem=sent, recv_sem=arrived, device_id=device, device_id_type=MESH
        ).start()

    def settle(ref, sem):
        pltpu.make_async_copy(ref, ref, sem).wait()

    loads = [
        pltpu.make_async_copy(scales_ref, scales_at, sem_in.at[5]),
        pltpu.make_async_copy(gain_ref, gain_at, sem_in.at[6]),
        pltpu.make_async_copy(nugget_ref, nugget_at, sem_in.at[7]),
        pltpu.make_async_copy(points_ref, px, sem_in.at[0]),
        pltpu.make_async_copy(ritz_ref, vf.at[0, 0, pl.ds(0, RITZ)], sem_in.at[1]),
        pltpu.make_async_copy(initial_ref, vf.at[0, 0, pl.ds(RITZ, RHS)], sem_in.at[2]),
        pltpu.make_async_copy(targets_ref, tgt, sem_in.at[3]),
        pltpu.make_async_copy(ritz_ref, wz.at[:, OWN * BLK :], sem_in.at[4]),
    ]
    for load in loads:
        load.start()
    barrier = pltpu.get_barrier_semaphore()
    for device in [d for _, _, d in along_z] + [d for _, _, d in plane[::-1]]:
        pl.semaphore_signal(barrier, inc=1, device_id=device, device_id_type=MESH)

    row = lax.broadcasted_iota(jnp.int32, (FEAT, BLK), 0)
    for load in loads[:4]:
        load.wait()
    gain = gain_at[0]
    nugget = nugget_at[0]
    scale = jnp.zeros((FEAT, BLK), F32)
    for i in range(FEAT):
        scale = jnp.where(row == i, scales_at[i], scale)
    scaled = px[...] * scale * math.sqrt(LOG2E)
    xf[0, 0] = scaled
    xz[OWN] = scaled
    for load in loads[4:]:
        load.wait()
    pl.semaphore_wait(barrier, NF - 1 + NZ - 1)

    for there, _, device in along_z:
        send(xz.at[OWN], xz.at[there], sxz, rxz, device)
    for k, device in same_core:
        send(xf.at[0, 0], xf.at[0, k], sx, rx, device)
    own_vec = vf.at[0, 0]
    own_w = wz.at[:, OWN * BLK :]

    def bulk():
        for k, device in same_core:
            send(own_vec, vf.at[0, k], sv, rv.at[k // HERE], device)
        for there, _, device in along_z:
            send(own_w, wz.at[:, there * BLK : (there + 1) * BLK], sw, rw, device)

    bulk()
    settle(xf.at[0, pl.ds(0, CHIPS - 1)], rx)
    send(xf.at[0], xf.at[1], sxf, rxf, other)

    def side(h):
        for k in range(CHIPS):
            at = (h * CHIPS + k) * BLK
            ljt[at : at + BLK, :] = features(xf[h, k], True).T.astype(BF16)

    def tile_rows(i):
        at = pl.ds(i * ROWS, ROWS)
        tile = jnp.exp2(jnp.minimum(fast(ljt[at, :], riz[...]), 0.0))
        high = tile.astype(BF16)
        khi[at, :] = high
        klo[at, :] = (tile - high.astype(F32)).astype(BF16)

    side(0)
    settle(xz.at[pl.ds(0, NZ - 1)], rxz)
    for o in range(NZ):
        riz[:, o * BLK : (o + 1) * BLK] = features(xz[o], False).astype(BF16)
    tile_rows(0)
    tile_rows(1)
    settle(xf.at[1], rxf)
    side(1)
    tile_rows(2)
    settle(vf.at[0, pl.ds(1, HERE - 1)], rv.at[0])
    send(vf.at[0, pl.ds(0, HERE)], vf.at[1, pl.ds(0, HERE)], svf.at[0], rvf.at[0], other)
    tile_rows(3)

    def vectors(h, near):
        for k in range(0 if near else HERE, HERE if near else CHIPS):
            high, mid, low = split3(vf[h, k])
            at = (h * CHIPS + k) * BLK
            v = jnp.concatenate([high, low[RITZ:], mid, jnp.zeros((PAD - VEC, BLK), F32)], axis=0)
            vcat[:, at : at + BLK] = v.astype(BF16)

    def product(h, near):
        vectors(h, near)
        at = pl.ds((h * CHIPS + (0 if near else HERE)) * BLK, HERE * BLK)
        a = fast(vcat[:, at], khi[at, :])
        b = fast(vcat[0:PAD, at], klo[at, :])
        low = jnp.concatenate([jnp.zeros((RITZ, NI), F32), a[VEC:PAD] + b[VEC:PAD]], axis=0)
        return a[0:VEC] + a[PAD : PAD + VEC] + b[0:VEC] + low

    part[...] = product(0, True)
    settle(vf.at[1, pl.ds(0, HERE)], rvf.at[0])
    part[...] = part[...] + product(1, True)
    settle(vf.at[0, pl.ds(HERE, HERE)], rv.at[1])
    send(vf.at[0, pl.ds(HERE, HERE)], vf.at[1, pl.ds(HERE, HERE)], svf.at[1], rvf.at[1], other)
    part[...] = part[...] + product(0, False)
    settle(vf.at[1, pl.ds(HERE, HERE)], rvf.at[1])
    part[...] = (part[...] + product(1, False)) * gain

    mine = part[:, OWN * BLK :] + nugget * own_vec[...]
    part[:, OWN * BLK :] = mine
    pin[z] = mine

    lane = lax.broadcasted_iota(jnp.int32, (RITZ, BLK), 1)
    settle(wz.at[:, pl.ds(0, (NZ - 1) * BLK)], rw)
    fill = jnp.zeros((BLK - VEC, NI), F32)
    coarse_part = matmul(wz[...], jnp.concatenate([part[...], fill], axis=0), ((1,), (1,)))
    ritz_own = own_vec[0:RITZ, :]
    start_own = own_vec[RITZ:VEC, :]
    target_rows = jnp.concatenate([jnp.zeros((RITZ, BLK), F32), tgt[...], jnp.zeros((BLK - VEC, BLK), F32)], axis=0)
    coarse_part = jnp.where(lane < RITZ, coarse_part, -coarse_part) + matmul(ritz_own, target_rows, ((1,), (1,)))
    ars[...] = coarse_part.reshape(NZ, RHS, BLK)
    for _, here, device in along_z:
        send(ars.at[zs[FAR[here]]], ara.at[z], sa, ra, device)
    for _, here, device in along_z:
        send(part.at[:, here * BLK : (here + 1) * BLK], pin.at[z], sp, rp, device)
    ara[z] = ars[z]
    settle(ara.at[pl.ds(0, NZ - 1)], ra)
    arb[f] = jnp.sum(ara[...], axis=0)
    for _, _, device in plane[::-1]:
        send(arb.at[f], arb.at[f], sb, rb, device)
    settle(arb.at[pl.ds(0, NF - 1)], rb)
    arc[z] = jnp.sum(arb[...], axis=0)
    for _, _, device in along_z:
        send(arc.at[z], arc.at[z], sc, rc, device)
    settle(arc.at[pl.ds(0, NZ - 1)], rc)
    first_sum = arc[...].reshape(RITZ, BLK)
    square = jnp.concatenate([first_sum, jnp.zeros((BLK - RITZ, BLK), F32)], axis=0)
    coarse = 0.5 * (first_sum + square.T[0:RITZ])
    sub = lax.broadcasted_iota(jnp.int32, (RITZ, BLK), 0)
    work = jnp.where(lane < RITZ, jnp.where(lane == sub, 1.0, 0.0), pltpu.roll(coarse, RITZ, 1))
    work = eliminate(work)
    inverse = work[:, 0:RITZ]
    amounts = matmul(inverse, first_sum, ((1,), (0,)))
    settle(pin.at[pl.ds(0, NZ - 1)], rp)
    image = jnp.sum(pin[...], axis=0)
    zimg = image[0:RITZ]
    r0 = tgt[...] - image[RITZ:VEC]
    wide = jnp.concatenate([ritz_own, zimg], axis=1)
    moved = matmul(amounts, wide, ((0,), (0,)))[RITZ:VEC]
    resid = r0 - moved[:, BLK:]
    rf[0, 0] = resid
    rz[OWN] = resid

    for k, o, device in plane[::-1]:
        send(rf.at[0, 0], rf.at[o, k], sr, rr.at[k // HERE], device)
    for there, _, device in along_z:
        send(rz.at[OWN], rz.at[there], srz, rrz, device)
    sol = start_own + moved[:, 0:BLK]
    lanes = lax.broadcasted_iota(jnp.int32, (RHS, BLK), 1)
    tall = jnp.concatenate([zimg, jnp.zeros((BLK - RITZ, BLK), F32)], axis=0)
    against = matmul(resid, tall, ((1,), (1,)))
    norm = jnp.sum(resid * resid, axis=1, keepdims=True)
    tz[z] = jnp.where(lanes < RITZ, against, jnp.where(lanes == RITZ, norm, 0.0))
    for _, _, device in along_z:
        send(tz.at[z], tz.at[z], stz, rtz, device)

    def second(near):
        total = None
        for h in range(NC):
            slots = range(0 if near else HERE, HERE if near else CHIPS)
            high, mid, low = split3(jnp.concatenate([rf[h, k] for k in slots], axis=1))
            v = jnp.concatenate([high, mid, low, jnp.zeros_like(high)], axis=0).astype(BF16)
            at = pl.ds((h * CHIPS + slots[0]) * BLK, HERE * BLK)
            a = fast(v, khi[at, :])
            b = fast(v[0:16], klo[at, :])
            one = a[0:8] + a[8:16] + a[16:24] + b[0:8] + b[8:16]
            total = one if total is None else total + one
        return total

    settle(rf.at[0, pl.ds(0, 2 * HERE - 1)], rr.at[0])
    acc[...] = second(True)
    settle(tz.at[pl.ds(0, NZ - 1)], rtz)
    tf[f] = jnp.sum(tz[...], axis=0)
    for _, _, device in plane[::-1]:
        send(tf.at[f], tf.at[f], st, rt, device)
    settle(rf.at[:, pl.ds(HERE, HERE)], rr.at[1])
    acc[...] = (acc[...] + second(False)) * gain
    settle(rz.at[pl.ds(0, NZ - 1)], rrz)
    acc[:, OWN * BLK :] = acc[:, OWN * BLK :] + nugget * resid
    curve = jnp.zeros((RHS, BLK), F32)
    for o in range(NZ):
        curve = curve + acc[:, o * BLK : (o + 1) * BLK] * rz[o]
    curve = jnp.sum(curve, axis=1, keepdims=True)
    here_lane = lanes == lax.broadcasted_iota(jnp.int32, (RHS, BLK), 0)
    gf[f] = jnp.sum(jnp.where(here_lane, curve, 0.0), axis=0, keepdims=True)
    for _, _, device in plane[::-1]:
        send(gf.at[f], gf.at[f], sg, rg, device)
    for _, here, device in along_z:
        send(acc.at[:, here * BLK : (here + 1) * BLK], fr.at[z], ss, rs, device)
    fr[z] = acc[:, OWN * BLK :]
    settle(gf.at[pl.ds(0, NF - 1)], rg)
    hz[z] = jnp.sum(gf[...], axis=0)
    for _, _, device in along_z:
        send(hz.at[z], hz.at[z], sh, rh, device)
    settle(tf.at[pl.ds(0, NF - 1)], rt)
    stats = jnp.sum(tf[...], axis=0)
    beta = matmul(stats[:, 0:RITZ], inverse, ((1,), (0,)))
    shift = matmul(beta, wide, ((1,), (0,)))
    direction = resid - shift[:, 0:BLK]
    deflated = jnp.sum(stats[:, 0:RITZ] * beta, axis=1, keepdims=True)
    settle(fr.at[pl.ds(0, NZ - 1)], rs)
    applied = jnp.sum(fr[...], axis=0) - shift[:, BLK:]
    settle(hz.at[pl.ds(0, NZ - 1)], rh)
    curve = jnp.sum(jnp.where(here_lane, jnp.sum(hz[...], axis=0), 0.0), axis=1, keepdims=True) - deflated
    step = stats[:, RITZ : RITZ + 1] / curve
    out_ref[0:RHS] = sol + step * direction
    out_ref[RHS:] = resid - step * applied

    settle(xf.at[0, pl.ds(0, CHIPS - 1)], sx)
    settle(xf.at[0], sxf)
    settle(xz.at[pl.ds(0, NZ - 1)], sxz)
    settle(vf.at[0, pl.ds(0, CHIPS - 1)], sv)
    for o in range(2):
        settle(vf.at[0, pl.ds(0, HERE)], svf.at[o])
    settle(wz.at[:, pl.ds(0, (NZ - 1) * BLK)], sw)
    settle(pin.at[pl.ds(0, NZ - 1)], sp)
    settle(ara.at[pl.ds(0, NZ - 1)], sa)
    settle(arb.at[pl.ds(0, NF - 1)], sb)
    settle(arc.at[pl.ds(0, NZ - 1)], sc)
    settle(rf.at[0, pl.ds(0, CHIPS - 1)], sr)
    settle(rf.at[1], sr)
    settle(rz.at[pl.ds(0, NZ - 1)], srz)
    settle(tz.at[pl.ds(0, NZ - 1)], stz)
    settle(fr.at[pl.ds(0, NZ - 1)], ss)
    settle(tf.at[pl.ds(0, NF - 1)], st)
    settle(gf.at[pl.ds(0, NF - 1)], sg)
    settle(hz.at[pl.ds(0, NZ - 1)], sh)


def local(points, inv_scales, amplitude, noise_var, targets, initial, ritz_basis):
    dma = pltpu.SemaphoreType.DMA
    hbm = pl.BlockSpec(memory_space=pltpu.HBM)
    vmem = pl.BlockSpec(memory_space=pltpu.VMEM)
    both = pl.pallas_call(
        body,
        out_shape=pltpu.VMEM((2 * RHS, BLK), F32),
        in_specs=[hbm, hbm, hbm, hbm, hbm, hbm, hbm],
        out_specs=vmem,
        scratch_shapes=[
            pltpu.SMEM((1,), F32),
            pltpu.SMEM((1,), F32),
            pltpu.SMEM((FEAT,), F32),
            pltpu.VMEM((FEAT, BLK), F32),
            pltpu.VMEM((NC, CHIPS, FEAT, BLK), F32),
            pltpu.VMEM((NZ, FEAT, BLK), F32),
            pltpu.VMEM((NC, CHIPS, VEC, BLK), F32),
            pltpu.VMEM((RITZ, NI), F32),
            pltpu.VMEM((RHS, BLK), F32),
            pltpu.VMEM((NJ, BLK), BF16),
            pltpu.VMEM((BLK, NI), BF16),
            pltpu.VMEM((NJ, NI), BF16),
            pltpu.VMEM((NJ, NI), BF16),
            pltpu.VMEM((2 * PAD, NJ), BF16),
            pltpu.VMEM((VEC, NI), F32),
            pltpu.VMEM((NZ, VEC, BLK), F32),
            pltpu.VMEM((NZ, RHS, BLK), F32),
            pltpu.VMEM((NZ, RHS, BLK), F32),
            pltpu.VMEM((NF, RHS, BLK), F32),
            pltpu.VMEM((NZ, RHS, BLK), F32),
            pltpu.VMEM((NC, CHIPS, RHS, BLK), F32),
            pltpu.VMEM((NZ, RHS, BLK), F32),
            pltpu.VMEM((NZ, RHS, BLK), F32),
            pltpu.VMEM((NF, RHS, BLK), F32),
            pltpu.VMEM((RHS, NI), F32),
            pltpu.VMEM((NZ, RHS, BLK), F32),
            pltpu.VMEM((NF, 1, BLK), F32),
            pltpu.VMEM((NZ, 1, BLK), F32),
            dma((8,)), dma, dma, dma, dma((2,)), dma((2,)), dma, dma, dma, dma, dma, dma((2,)), dma, dma, dma, dma, dma, dma,
            dma, dma, dma, dma, dma((2,)), dma, dma, dma, dma, dma, dma, dma, dma, dma, dma, dma, dma,
        ],
        compiler_params=pltpu.CompilerParams(
            collective_id=0, has_side_effects=True, vmem_limit_bytes=60 * 1024 * 1024
        ),
    )(amplitude, noise_var, inv_scales, points, targets, initial, ritz_basis)
    return both[:RHS], both[RHS:]


def solution(mesh):
    torus = Mesh(mesh.devices.reshape(NY, NZ, NX, NC), ("row_0", "row_1", "col_0", "col_1"))
    split = P(None, ("col_0", "col_1", "row_0", "row_1"))
    return jax.shard_map(
        local,
        mesh=torus,
        in_specs=(split, P(), P(), P(), split, split, split),
        out_specs=(split, split),
        check_vma=False,
    )
```

time: 69.7 us -> 63.1 us (0.905)
  Pallas kernels: 65.7 us -> 60.4 us
  local copies, waits for them, and re-layouts: 1.86 us -> 0.6 us
    pallas_call x1, Pallas kernels: 65.7 us -> 60.4 us  [local(): pl.pallas_call(body, out_shape=pltpu.VMEM((2 * RHS, BLK), F32), in_specs=...]
    unnamed x4 -> x0, local copies, waits for them, and re-layouts: 1.86 us -> none
where the time goes in v3:
time: 63.1 us; the launch traced here: 63 us
  Pallas kernels  60.4 us (96%)
  between operations  1.93 us (3%)
    pallas_call x1, Pallas kernels, local(): pl.pallas_call(body, out_shape=pltpu.VMEM((2 * RHS, BLK), F32), in_specs=...  60.4 us

profile of v3, /device:TPU:1, one launch (start us, length us, event | category | flops | bytes accessed | tf_op | source)
XLA Modules:
  0.0 63.0 jit_solution(6103169375297410419)
XLA Ops:
  1.9 60.4 %shard_map.86 = f32[16,128]{1,0:T(8,128)S(1)} custom-call(f32[1]{0:T(128)S(6)} %copy.9.gain_ref, f32[1]{0:T(128)S(6)} %copy.10.nugget_ref, f32[16]{0:T(128)} %scales_ref.1, f32[16,128]{1,0:T(8,128)} %points_ref.1, f32[8,128]{1,0:T(8,128)} %targets_ref.1, f32[8,128]{1,0:T(8,128)} %initial_ref.1, f32[64,128]{1,0:T(8,128)} %ritz_ref.1), custom_call_target="tpu_custom_call" | custom-call | tf_op jit(solution)/shard_map/pallas_call | solution.py:377
  62.4 0.6 fusion

commit v4 on v3

--- a/solution.py
+++ b/solution.py
@@ -171,8 +171,10 @@
     xz[OWN] = scaled
     for load in loads[4:]:
         load.wait()
+    pl.delay(1)
     pl.semaphore_wait(barrier, NF - 1 + NZ - 1)
 
+    pl.delay(1)
     for there, _, device in along_z:
         send(xz.at[OWN], xz.at[there], sxz, rxz, device)
     for k, device in same_core:
@@ -187,6 +189,7 @@
             send(own_w, wz.at[:, there * BLK : (there + 1) * BLK], sw, rw, device)
 
     bulk()
+    pl.delay(1)
     settle(xf.at[0, pl.ds(0, CHIPS - 1)], rx)
     send(xf.at[0], xf.at[1], sxf, rxf, other)
 
@@ -197,22 +200,32 @@
 
     def tile_rows(i):
         at = pl.ds(i * ROWS, ROWS)
-        tile = jnp.exp2(jnp.minimum(fast(ljt[at, :], riz[...]), 0.0))
-        high = tile.astype(BF16)
-        khi[at, :] = high
-        klo[at, :] = (tile - high.astype(F32)).astype(BF16)
-
+        for to in (pl.ds(0, NI // 2), pl.ds(NI // 2, NI // 2)):
+            tile = jnp.exp2(jnp.minimum(fast(ljt[at, :], riz[:, to]), 0.0))
+            high = tile.astype(BF16)
+            khi[at, to] = high
+            klo[at, to] = (tile - high.astype(F32)).astype(BF16)
+
+    pl.delay(1)
     side(0)
+    pl.delay(1)
     settle(xz.at[pl.ds(0, NZ - 1)], rxz)
+    pl.delay(1)
     for o in range(NZ):
         riz[:, o * BLK : (o + 1) * BLK] = features(xz[o], False).astype(BF16)
+    pl.delay(1)
     tile_rows(0)
     tile_rows(1)
+    pl.delay(1)
     settle(xf.at[1], rxf)
+    pl.delay(1)
     side(1)
+    pl.delay(1)
     tile_rows(2)
+    pl.delay(1)
     settle(vf.at[0, pl.ds(1, HERE - 1)], rv.at[0])
     send(vf.at[0, pl.ds(0, HERE)], vf.at[1, pl.ds(0, HERE)], svf.at[0], rvf.at[0], other)
+    pl.delay(1)
     tile_rows(3)
 
     def vectors(h, near):
@@ -230,21 +243,31 @@
         low = jnp.concatenate([jnp.zeros((RITZ, NI), F32), a[VEC:PAD] + b[VEC:PAD]], axis=0)
         return a[0:VEC] + a[PAD : PAD + VEC] + b[0:VEC] + low
 
+    pl.delay(1)
     part[...] = product(0, True)
+    pl.delay(1)
     settle(vf.at[1, pl.ds(0, HERE)], rvf.at[0])
+    pl.delay(1)
     part[...] = part[...] + product(1, True)
+    pl.delay(1)
     settle(vf.at[0, pl.ds(HERE, HERE)], rv.at[1])
     send(vf.at[0, pl.ds(HERE, HERE)], vf.at[1, pl.ds(HERE, HERE)], svf.at[1], rvf.at[1], other)
+    pl.delay(1)
     part[...] = part[...] + product(0, False)
+    pl.delay(1)
     settle(vf.at[1, pl.ds(HERE, HERE)], rvf.at[1])
+    pl.delay(1)
     part[...] = (part[...] + product(1, False)) * gain
 
+    pl.delay(1)
     mine = part[:, OWN * BLK :] + nugget * own_vec[...]
     part[:, OWN * BLK :] = mine
     pin[z] = mine
 
     lane = lax.broadcasted_iota(jnp.int32, (RITZ, BLK), 1)
+    pl.delay(1)
     settle(wz.at[:, pl.ds(0, (NZ - 1) * BLK)], rw)
+    pl.delay(1)
     fill = jnp.zeros((BLK - VEC, NI), F32)
     coarse_part = matmul(wz[...], jnp.concatenate([part[...], fill], axis=0), ((1,), (1,)))
     ritz_own = own_vec[0:RITZ, :]
@@ -257,15 +280,19 @@
     for _, here, device in along_z:
         send(part.at[:, here * BLK : (here + 1) * BLK], pin.at[z], sp, rp, device)
     ara[z] = ars[z]
+    pl.delay(1)
     settle(ara.at[pl.ds(0, NZ - 1)], ra)
     arb[f] = jnp.sum(ara[...], axis=0)
     for _, _, device in plane[::-1]:
         send(arb.at[f], arb.at[f], sb, rb, device)
+    pl.delay(1)
     settle(arb.at[pl.ds(0, NF - 1)], rb)
     arc[z] = jnp.sum(arb[...], axis=0)
     for _, _, device in along_z:
         send(arc.at[z], arc.at[z], sc, rc, device)
+    pl.delay(1)
     settle(arc.at[pl.ds(0, NZ - 1)], rc)
+    pl.delay(1)
     first_sum = arc[...].reshape(RITZ, BLK)
     square = jnp.concatenate([first_sum, jnp.zeros((BLK - RITZ, BLK), F32)], axis=0)
     coarse = 0.5 * (first_sum + square.T[0:RITZ])
@@ -273,21 +300,26 @@
     work = jnp.where(lane < RITZ, jnp.where(lane == sub, 1.0, 0.0), pltpu.roll(coarse, RITZ, 1))
     work = eliminate(work)
     inverse = work[:, 0:RITZ]
+    pl.delay(1)
     amounts = matmul(inverse, first_sum, ((1,), (0,)))
+    pl.delay(1)
     settle(pin.at[pl.ds(0, NZ - 1)], rp)
     image = jnp.sum(pin[...], axis=0)
     zimg = image[0:RITZ]
     r0 = tgt[...] - image[RITZ:VEC]
+    pl.delay(1)
     wide = jnp.concatenate([ritz_own, zimg], axis=1)
     moved = matmul(amounts, wide, ((0,), (0,)))[RITZ:VEC]
     resid = r0 - moved[:, BLK:]
     rf[0, 0] = resid
     rz[OWN] = resid
 
+    pl.delay(1)
     for k, o, device in plane[::-1]:
         send(rf.at[0, 0], rf.at[o, k], sr, rr.at[k // HERE], device)
     for there, _, device in along_z:
         send(rz.at[OWN], rz.at[there], srz, rrz, device)
+    pl.delay(1)
     sol = start_own + moved[:, 0:BLK]
     lanes = lax.broadcasted_iota(jnp.int32, (RHS, BLK), 1)
     tall = jnp.concatenate([zimg, jnp.zeros((BLK - RITZ, BLK), F32)], axis=0)
@@ -310,15 +342,21 @@
             total = one if total is None else total + one
         return total
 
+    pl.delay(1)
     settle(rf.at[0, pl.ds(0, 2 * HERE - 1)], rr.at[0])
+    pl.delay(1)
     acc[...] = second(True)
     settle(tz.at[pl.ds(0, NZ - 1)], rtz)
     tf[f] = jnp.sum(tz[...], axis=0)
     for _, _, device in plane[::-1]:
         send(tf.at[f], tf.at[f], st, rt, device)
+    pl.delay(1)
     settle(rf.at[:, pl.ds(HERE, HERE)], rr.at[1])
+    pl.delay(1)
     acc[...] = (acc[...] + second(False)) * gain
+    pl.delay(1)
     settle(rz.at[pl.ds(0, NZ - 1)], rrz)
+    pl.delay(1)
     acc[:, OWN * BLK :] = acc[:, OWN * BLK :] + nugget * resid
     curve = jnp.zeros((RHS, BLK), F32)
     for o in range(NZ):
@@ -331,10 +369,13 @@
     for _, here, device in along_z:
         send(acc.at[:, here * BLK : (here + 1) * BLK], fr.at[z], ss, rs, device)
     fr[z] = acc[:, OWN * BLK :]
+    pl.delay(1)
     settle(gf.at[pl.ds(0, NF - 1)], rg)
+    pl.delay(1)
     hz[z] = jnp.sum(gf[...], axis=0)
     for _, _, device in along_z:
         send(hz.at[z], hz.at[z], sh, rh, device)
+    pl.delay(1)
     settle(tf.at[pl.ds(0, NF - 1)], rt)
     stats = jnp.sum(tf[...], axis=0)
     beta = matmul(stats[:, 0:RITZ], inverse, ((1,), (0,)))
@@ -343,12 +384,15 @@
     deflated = jnp.sum(stats[:, 0:RITZ] * beta, axis=1, keepdims=True)
     settle(fr.at[pl.ds(0, NZ - 1)], rs)
     applied = jnp.sum(fr[...], axis=0) - shift[:, BLK:]
+    pl.delay(1)
     settle(hz.at[pl.ds(0, NZ - 1)], rh)
+    pl.delay(1)
     curve = jnp.sum(jnp.where(here_lane, jnp.sum(hz[...], axis=0), 0.0), axis=1, keepdims=True) - deflated
     step = stats[:, RITZ : RITZ + 1] / curve
     out_ref[0:RHS] = sol + step * direction
     out_ref[RHS:] = resid - step * applied
 
+    pl.delay(1)
     settle(xf.at[0, pl.ds(0, CHIPS - 1)], sx)
     settle(xf.at[0], sxf)
     settle(xz.at[pl.ds(0, NZ - 1)], sxz)

time: 63.1 us -> 61.8 us (0.979)
  Pallas kernels: 60.4 us -> 59.1 us
    pallas_call x1, Pallas kernels: 60.4 us -> 59.1 us  [local(): pl.pallas_call(body, out_shape=pltpu.VMEM((2 * RHS, BLK), F32), in_specs=...]
where the time goes in v4:
time: 61.8 us; the launch traced here: 61.6 us
  Pallas kernels  59.1 us (96%)
  between operations  1.93 us (3%)
    pallas_call x1, Pallas kernels, local(): pl.pallas_call(body, out_shape=pltpu.VMEM((2 * RHS, BLK), F32), in_specs=...  59.1 us

profile of v4, /device:TPU:1, one launch (start us, length us, event | category | flops | bytes accessed | tf_op | source)
XLA Modules:
  0.0 61.6 jit_solution(11681720948243982869)
XLA Ops:
  1.9 59.1 %shard_map.86 = f32[16,128]{1,0:T(8,128)S(1)} custom-call(f32[1]{0:T(128)S(6)} %copy.9.gain_ref, f32[1]{0:T(128)S(6)} %copy.10.nugget_ref, f32[16]{0:T(128)} %scales_ref.1, f32[16,128]{1,0:T(8,128)} %points_ref.1, f32[8,128]{1,0:T(8,128)} %targets_ref.1, f32[8,128]{1,0:T(8,128)} %initial_ref.1, f32[64,128]{1,0:T(8,128)} %ritz_ref.1), custom_call_target="tpu_custom_call" | custom-call | tf_op jit(solution)/shard_map/pallas_call | solution.py:421
  61.0 0.6 fusion

commit v5 on v4

--- a/solution.py
+++ b/solution.py
@@ -295,13 +295,15 @@
     pl.delay(1)
     first_sum = arc[...].reshape(RITZ, BLK)
     square = jnp.concatenate([first_sum, jnp.zeros((BLK - RITZ, BLK), F32)], axis=0)
-    coarse = 0.5 * (first_sum + square.T[0:RITZ])
+    turned = square.T
+    coarse = 0.5 * (first_sum + turned[0:RITZ])
+    projected = turned[RITZ:VEC, 0:RITZ]
     sub = lax.broadcasted_iota(jnp.int32, (RITZ, BLK), 0)
     work = jnp.where(lane < RITZ, jnp.where(lane == sub, 1.0, 0.0), pltpu.roll(coarse, RITZ, 1))
     work = eliminate(work)
     inverse = work[:, 0:RITZ]
     pl.delay(1)
-    amounts = matmul(inverse, first_sum, ((1,), (0,)))
+    amounts = matmul(projected, inverse, ((1,), (0,)))
     pl.delay(1)
     settle(pin.at[pl.ds(0, NZ - 1)], rp)
     image = jnp.sum(pin[...], axis=0)
@@ -309,14 +311,14 @@
     r0 = tgt[...] - image[RITZ:VEC]
     pl.delay(1)
     wide = jnp.concatenate([ritz_own, zimg], axis=1)
-    moved = matmul(amounts, wide, ((0,), (0,)))[RITZ:VEC]
+    moved = matmul(amounts, wide, ((1,), (0,)))
     resid = r0 - moved[:, BLK:]
-    rf[0, 0] = resid
+    rf[0] = resid
     rz[OWN] = resid
 
     pl.delay(1)
     for k, o, device in plane[::-1]:
-        send(rf.at[0, 0], rf.at[o, k], sr, rr.at[k // HERE], device)
+        send(rf.at[0], rf.at[o * CHIPS + k], sr, rr, device)
     for there, _, device in along_z:
         send(rz.at[OWN], rz.at[there], srz, rrz, device)
     pl.delay(1)
@@ -329,31 +331,14 @@
     for _, _, device in along_z:
         send(tz.at[z], tz.at[z], stz, rtz, device)
 
-    def second(near):
-        total = None
-        for h in range(NC):
-            slots = range(0 if near else HERE, HERE if near else CHIPS)
-            high, mid, low = split3(jnp.concatenate([rf[h, k] for k in slots], axis=1))
-            v = jnp.concatenate([high, mid, low, jnp.zeros_like(high)], axis=0).astype(BF16)
-            at = pl.ds((h * CHIPS + slots[0]) * BLK, HERE * BLK)
-            a = fast(v, khi[at, :])
-            b = fast(v[0:16], klo[at, :])
-            one = a[0:8] + a[8:16] + a[16:24] + b[0:8] + b[8:16]
-            total = one if total is None else total + one
-        return total
-
-    pl.delay(1)
-    settle(rf.at[0, pl.ds(0, 2 * HERE - 1)], rr.at[0])
-    pl.delay(1)
-    acc[...] = second(True)
-    settle(tz.at[pl.ds(0, NZ - 1)], rtz)
-    tf[f] = jnp.sum(tz[...], axis=0)
-    for _, _, device in plane[::-1]:
-        send(tf.at[f], tf.at[f], st, rt, device)
-    pl.delay(1)
-    settle(rf.at[:, pl.ds(HERE, HERE)], rr.at[1])
-    pl.delay(1)
-    acc[...] = (acc[...] + second(False)) * gain
+    pl.delay(1)
+    settle(rf.at[pl.ds(0, NF - 1)], rr)
+    pl.delay(1)
+    high, mid, low = split3(jnp.concatenate([rf[k] for k in range(NF)], axis=1))
+    v = jnp.concatenate([high, mid, low, jnp.zeros_like(high)], axis=0).astype(BF16)
+    a = fast(v, khi[...])
+    b = fast(v[0:16], klo[...])
+    acc[...] = (a[0:8] + a[8:16] + a[16:24] + b[0:8] + b[8:16]) * gain
     pl.delay(1)
     settle(rz.at[pl.ds(0, NZ - 1)], rrz)
     pl.delay(1)
@@ -370,6 +355,11 @@
         send(acc.at[:, here * BLK : (here + 1) * BLK], fr.at[z], ss, rs, device)
     fr[z] = acc[:, OWN * BLK :]
     pl.delay(1)
+    settle(tz.at[pl.ds(0, NZ - 1)], rtz)
+    tf[f] = jnp.sum(tz[...], axis=0)
+    for _, _, device in plane[::-1]:
+        send(tf.at[f], tf.at[f], st, rt, device)
+    pl.delay(1)
     settle(gf.at[pl.ds(0, NF - 1)], rg)
     pl.delay(1)
     hz[z] = jnp.sum(gf[...], axis=0)
@@ -404,8 +394,7 @@
     settle(ara.at[pl.ds(0, NZ - 1)], sa)
     settle(arb.at[pl.ds(0, NF - 1)], sb)
     settle(arc.at[pl.ds(0, NZ - 1)], sc)
-    settle(rf.at[0, pl.ds(0, CHIPS - 1)], sr)
-    settle(rf.at[1], sr)
+    settle(rf.at[pl.ds(0, NF - 1)], sr)
     settle(rz.at[pl.ds(0, NZ - 1)], srz)
     settle(tz.at[pl.ds(0, NZ - 1)], stz)
     settle(fr.at[pl.ds(0, NZ - 1)], ss)
@@ -444,7 +433,7 @@
             pltpu.VMEM((NZ, RHS, BLK), F32),
             pltpu.VMEM((NF, RHS, BLK), F32),
             pltpu.VMEM((NZ, RHS, BLK), F32),
-            pltpu.VMEM((NC, CHIPS, RHS, BLK), F32),
+            pltpu.VMEM((NF, RHS, BLK), F32),
             pltpu.VMEM((NZ, RHS, BLK), F32),
             pltpu.VMEM((NZ, RHS, BLK), F32),
             pltpu.VMEM((NF, RHS, BLK), F32),
@@ -452,7 +441,7 @@
             pltpu.VMEM((NZ, RHS, BLK), F32),
             pltpu.VMEM((NF, 1, BLK), F32),
             pltpu.VMEM((NZ, 1, BLK), F32),
-            dma((8,)), dma, dma, dma, dma((2,)), dma((2,)), dma, dma, dma, dma, dma, dma((2,)), dma, dma, dma, dma, dma, dma,
+            dma((8,)), dma, dma, dma, dma((2,)), dma((2,)), dma, dma, dma, dma, dma, dma, dma, dma, dma, dma, dma, dma,
             dma, dma, dma, dma, dma((2,)), dma, dma, dma, dma, dma, dma, dma, dma, dma, dma, dma, dma,
         ],
         compiler_params=pltpu.CompilerParams(

time: 61.8 us -> 62.1 us (level)
  no operation moved by 1% of the time
where the time goes in v5:
time: 62.1 us; the launch traced here: 61.9 us
  Pallas kernels  59.4 us (96%)
  between operations  1.93 us (3%)
    pallas_call x1, Pallas kernels, local(): pl.pallas_call(body, out_shape=pltpu.VMEM((2 * RHS, BLK), F32), in_specs=...  59.4 us

profile of v5, /device:TPU:1, one launch (start us, length us, event | category | flops | bytes accessed | tf_op | source)
XLA Modules:
  0.0 61.9 jit_solution(488465673167045254)
XLA Ops:
  1.9 59.4 %shard_map.86 = f32[16,128]{1,0:T(8,128)S(1)} custom-call(f32[1]{0:T(128)S(6)} %copy.9.gain_ref, f32[1]{0:T(128)S(6)} %copy.10.nugget_ref, f32[16]{0:T(128)} %scales_ref.1, f32[16,128]{1,0:T(8,128)} %points_ref.1, f32[8,128]{1,0:T(8,128)} %targets_ref.1, f32[8,128]{1,0:T(8,128)} %initial_ref.1, f32[64,128]{1,0:T(8,128)} %ritz_ref.1), custom_call_target="tpu_custom_call" | custom-call | tf_op jit(solution)/shard_map/pallas_call | solution.py:410
  61.3 0.6 fusion
